TPU v7x, 128 devices: a whole 4x4x4 slice. The times are simulated.
128 devices in a mesh: gx: 8 (over y, core), gy: 16 (over z, x).
Axes of the slice: x: 4, y: 4, z: 4, core: 2. Of those that a mesh axis runs over, the one named last changes fastest.
Arguments:
- weighted_jacobian_strips: float32 [16384, 3, 768], P(('gx', 'gy')), may hold values from -0.3125 to 0.3125
- leading_pose_index: int32 [16384, 1], P(('gx', 'gy')), may hold values from 0 to 127; in each aligned block of 128 rows (0 to 127, 128 to 255, ...) at most 2 rows name the same one
- levenberg_shift: float32 [128, 768], P(('gx', 'gy')), may hold values from 0.05 to 0.5
- removal_flags: int32 [128], replicated, may hold values from 0 to 1, as said below
Outputs:
- schur: float32 [128, 3, 768, 768], P(('gx', 'gy'))
- coupling: float32 [128, 4, 768, 768], P(('gx', 'gy'))
Inputs may be any that keep to these rules, and one draw needn't show every extreme that they name: `leading_pose_index`: within the 128 columns of one device no block is the base of more than 2 columns, and some device reaches 2. `removal_flags`: eliminated blocks lie 3 or more blocks apart around the cycle of 128 blocks.
All inputs are finite; a program needn't handle non-finite values.
Results may differ from a plain program's by a relative error of at most 0.0003.
Values sent between devices are 32-bit elements; how exact they have to be, the bound alone decides.
A program may use at most 192 MiB of HBM per device.

v0:
```python
import jax
import jax.numpy as jnp
from jax import lax
from jax.sharding import PartitionSpec as P


def passed_along(value, axis, steps):
    count = lax.axis_size(axis)
    pairs = [(source, (source + steps) % count) for source in range(count)]
    return lax.ppermute(value, axis, pairs)


def gram_product(left_op, right_op):
    return lax.dot_general(
        left_op,
        right_op,
        (((0,), (0,)), ((), ())),
        precision=lax.Precision.HIGHEST,
        preferred_element_type=jnp.float32,
    )


def local(weighted_jacobian_strips, leading_pose_index, levenberg_shift, removal_flags):
    block_count = lax.axis_size(("gx", "gy"))
    own_block = lax.axis_index(("gx", "gy"))
    surfels = weighted_jacobian_strips.shape[0]
    block_rows = weighted_jacobian_strips.shape[2]
    capacity = max(2, (3 * surfels + 2 * block_count - 1) // (2 * block_count))
    blocks = leading_pose_index[:, 0]
    onehot = (blocks[:, None] == jnp.arange(block_count, dtype=jnp.int32)[None, :]).astype(
        jnp.int32
    )
    earlier = jnp.cumsum(onehot, axis=0) - onehot
    within = jnp.sum(earlier * onehot, axis=1)
    target = blocks * capacity + within
    bucket = jnp.zeros((block_count * capacity, 3 * block_rows), jnp.float32)
    bucket = bucket.at[target].set(weighted_jacobian_strips.reshape(surfels, 3 * block_rows))
    bucket = bucket.reshape(block_count, capacity, 3, block_rows)
    counts = (1, 2, 3)
    payload = jnp.concatenate(
        [
            jnp.roll(bucket[:, :, : counts[offset], :], offset, axis=0).reshape(
                block_count, capacity, counts[offset] * block_rows
            )
            for offset in range(3)
        ],
        axis=2,
    )
    lane_count = payload.shape[2]
    incoming_block = lax.all_to_all(
        payload.reshape(block_count * capacity, lane_count),
        ("gx", "gy"),
        split_axis=0,
        concat_axis=0,
        tiled=True,
    )
    starts = (0, counts[0], counts[0] + counts[1])

    def piece_of(offset, member):
        begin_at = (starts[offset] + member) * block_rows
        return incoming_block[:, begin_at : begin_at + block_rows]

    diag_tile = gram_product(piece_of(0, 0), piece_of(0, 0)) + gram_product(
        piece_of(1, 1), piece_of(1, 1)
    )
    diag_tile = (
        diag_tile + gram_product(piece_of(2, 2), piece_of(2, 2)) + jnp.diag(levenberg_shift[0])
    )
    near_tile = gram_product(piece_of(1, 0), piece_of(1, 1)) + gram_product(
        piece_of(2, 1), piece_of(2, 2)
    )
    far_tile = gram_product(piece_of(2, 0), piece_of(2, 2))
    fetched = [
        passed_along(tile_in, ("gx", "gy"), step)
        for step, tile_in in ((-1, near_tile), (-2, far_tile))
    ]
    next_tile = fetched[0]
    after_tile = fetched[1]
    factor = jnp.linalg.cholesky(diag_tile)
    right_sides = jnp.concatenate([far_tile.T, near_tile.T, next_tile, after_tile], axis=1)
    solved = jax.scipy.linalg.solve_triangular(factor, right_sides, lower=True)
    panels = [solved[:, member * block_rows : (member + 1) * block_rows] for member in range(4)]
    flag_strip = removal_flags.astype(jnp.float32)

    def flag_at(shift_by):
        return lax.dynamic_index_in_dim(
            flag_strip, (own_block + shift_by) % block_count, keepdims=False
        )

    own_flag = flag_at(0)
    incoming = [
        passed_along(jnp.stack(coupling_term), ("gx", "gy"), step)
        for step, coupling_term in (
            (2, (panels[2], panels[3])),
            (1, (panels[1], panels[2])),
            (-1, (panels[0], panels[1])),
        )
    ]
    from_two_below = incoming[0]
    from_one_below = incoming[1]
    from_one_above = incoming[2]
    from_two_above = passed_along(panels[0], ("gx", "gy"), -2)
    flag_two_above = flag_at(2)
    flag_one_above = flag_at(1)
    flag_one_below = flag_at(-1)
    flag_two_below = flag_at(-2)
    new_diag = diag_tile - flag_two_above * gram_product(from_two_above, from_two_above)
    new_diag = new_diag - flag_one_above * gram_product(from_one_above[1], from_one_above[1])
    new_diag = new_diag - flag_one_below * gram_product(from_one_below[1], from_one_below[1])
    new_diag = new_diag - flag_two_below * gram_product(from_two_below[1], from_two_below[1])
    new_near = near_tile - flag_one_above * gram_product(from_one_above[0], from_one_above[1])
    new_near = new_near - flag_two_below * gram_product(from_two_below[0], from_two_below[1])
    new_far = far_tile - flag_one_below * gram_product(from_one_below[0], from_one_below[1])
    new_near = jnp.where(flag_one_below > 0, from_one_below[1], new_near)
    new_far = jnp.where(flag_two_below > 0, from_two_below[1], new_far)
    current_pose_tile = own_flag > 0
    schur = jnp.stack(
        [
            jnp.where(current_pose_tile, panels[0].T, new_far),
            jnp.where(current_pose_tile, panels[1].T, new_near),
            jnp.where(current_pose_tile, factor, new_diag),
        ]
    )
    coupling = jnp.stack([from_two_above, from_one_above[1], from_one_below[1], from_two_below[1]])
    return (schur[None], coupling[None])


def solution(mesh):
    in_specs = (P(("gx", "gy"), None, None), P(("gx", "gy"), None), P(("gx", "gy"), None), P())
    out_specs = (P(("gx", "gy"), None, None, None), P(("gx", "gy"), None, None, None))
    return jax.shard_map(local, mesh=mesh, in_specs=in_specs, out_specs=out_specs, check_vma=False)
```

profile of v0, /device:TPU:0, one launch (start us, length us, event | category | flops | bytes accessed | tf_op | source)
XLA Modules:
  0.0 829.9 jit_solution(10559810097351764612)
XLA Ops:
  10.4 3.6 slice.303
  23.6 6.3 maximum_maximum_fusion
  29.9 11.8 %all-to-all-start = ((f32[128,2,4608]{2,1,0:T(2,128)}), f32[128,2,4608]{2,1,0:T(2,128)}, u32[]{:S(2)}, u32[]{:S(2)}) async-start(f32[128,2,4608]{2,1,0:T(2,128)} %maximum_maximum_fusion), calls=%async_computation | async-start | bytes 9437184 | tf_op jit(solution)/shard_map/all_to_all | solution.py:50
  41.8 56.1 %all-to-all-done = f32[128,2,4608]{2,1,0:T(2,128)} async-done(((f32[128,2,4608]{2,1,0:T(2,128)}), f32[128,2,4608]{2,1,0:T(2,128)}, u32[]{:S(2)}, u32[]{:S(2)}) %all-to-all-start) | async-done | bytes 4718624 | tf_op jit(solution)/shard_map/all_to_all | solution.py:50
  98.0 6.5 all_to_all.7
  104.5 5.0 fusion.38
  109.5 4.8 fusion.36
  127.0 11.7 %cholesky.166 = f32[128,128]{1,0:T(8,128)S(1)} custom-call(f32[128,128]{1,0:T(8,128)S(1)} %cholesky.424), custom_call_target="Cholesky" | custom-call | tf_op jit(solution)/shard_map/jit(cholesky)/cholesky | solution.py:79
  138.9 5.6 convolution_add_fusion
  155.0 9.8 %custom-call.47 = f32[1,128,128]{1,2,0:T(8,128)S(1)} custom-call(f32[1,128,128]{2,1,0:T(8,128)S(1)} %get-tuple-element.55), custom_call_target="InvertDiagBlocksLowerTriangular" | custom-call | tf_op jit(solution)/shard_map/jit(cholesky)/cholesky | solution.py:79
  167.6 11.7 %cholesky.189 = f32[128,128]{1,0:T(8,128)S(1)} custom-call(f32[128,128]{1,0:T(8,128)S(1)} %cholesky.428), custom_call_target="Cholesky" | custom-call | tf_op jit(solution)/shard_map/jit(cholesky)/cholesky | solution.py:79
  179.4 9.8 %custom-call.48 = f32[1,128,128]{1,2,0:T(8,128)S(1)} custom-call(f32[1,128,128]{2,1,0:T(8,128)S(1)} %get-tuple-element.52), custom_call_target="InvertDiagBlocksLowerTriangular" | custom-call | tf_op jit(solution)/shard_map/jit(cholesky)/cholesky | solution.py:79
  191.1 11.9 %cholesky.355 = f32[128,128]{1,0:T(8,128)S(1)} custom-call(f32[128,128]{1,0:T(8,128)S(1)} %cholesky.433), custom_call_target="Cholesky" | custom-call | tf_op jit(solution)/shard_map/jit(cholesky)/cholesky | solution.py:79
  203.7 9.8 %custom-call.49 = f32[1,128,128]{1,2,0:T(8,128)S(1)} custom-call(f32[1,128,128]{2,1,0:T(8,128)S(1)} %get-tuple-element.49), custom_call_target="InvertDiagBlocksLowerTriangular" | custom-call | tf_op jit(solution)/shard_map/jit(cholesky)/cholesky | solution.py:79
  215.4 11.7 %cholesky.374 = f32[128,128]{1,0:T(8,128)S(1)} custom-call(f32[128,128]{1,0:T(8,128)S(1)} %cholesky.438), custom_call_target="Cholesky" | custom-call | tf_op jit(solution)/shard_map/jit(cholesky)/cholesky | solution.py:79
  227.8 9.8 %custom-call.50 = f32[1,128,128]{1,2,0:T(8,128)S(1)} custom-call(f32[1,128,128]{2,1,0:T(8,128)S(1)} %get-tuple-element.46), custom_call_target="InvertDiagBlocksLowerTriangular" | custom-call | tf_op jit(solution)/shard_map/jit(cholesky)/cholesky | solution.py:79
  239.4 12.1 %cholesky.393 = f32[128,128]{1,0:T(8,128)S(1)} custom-call(f32[128,128]{1,0:T(8,128)S(1)} %cholesky.443), custom_call_target="Cholesky" | custom-call | tf_op jit(solution)/shard_map/jit(cholesky)/cholesky | solution.py:79
  252.2 9.8 %custom-call.51 = f32[1,128,128]{1,2,0:T(8,128)S(1)} custom-call(f32[1,128,128]{2,1,0:T(8,128)S(1)} %get-tuple-element.43), custom_call_target="InvertDiagBlocksLowerTriangular" | custom-call | tf_op jit(solution)/shard_map/jit(cholesky)/cholesky | solution.py:79
  263.6 11.7 %cholesky.411 = f32[128,128]{1,0:T(8,128)S(1)} custom-call(f32[128,128]{1,0:T(8,128)S(1)} %convolution_subtract_fusion.4), custom_call_target="Cholesky" | custom-call | tf_op jit(solution)/shard_map/jit(cholesky)/cholesky | solution.py:79
  282.2 17.9 %while.1 = (s32[]{:T(128)}, f32[768,768]{1,0:T(8,128)}, s32[6,2]{0,1:T(2,128)S(1)}, f32[6,128,128]{2,1,0:T(8,128)S(1)}, s32[]{:T(128)}) while((s32[]{:T(128)}, f32[768,768]{1,0:T(8,128)}, s32[6,2]{0,1:T(2,128)S(1)}, f32[6,128,128]{2,1,0:T(8,128)S(1)}, s32[]{:T(128)}) %tuple.56), condition=%wide.while_cond, body=%wide.while_body.sunk | while | flops 2 | bytes 131189 | solution.py:81
  300.1 59.0 %custom-call.52 = f32[6,128,128]{1,2,0:T(8,128)S(1)} custom-call(f32[6,128,128]{2,1,0:T(8,128)S(1)} %get-tuple-element.9), custom_call_target="InvertDiagBlocksLowerTriangular" | custom-call | tf_op jit(solution)/shard_map/jit(_solve_triangular)/triangular_solve | solution.py:81
  359.1 4.6 pad_maximum_fusion
  363.6 3.7 copy-done.1
  376.4 4.6 constant_dynamic-update-slice_fusion.3
  384.1 3.7 fusion.14
  387.9 4.6 constant_dynamic-update-slice_fusion.2
  395.5 4.8 fusion.8
  400.3 4.2 constant_dynamic-update-slice_fusion.1
  405.7 6.1 fusion
  414.8 5.0 constant_dynamic-update-slice_fusion
  419.8 9.0 %fusion.51 = f32[128,3072]{1,0:T(8,128)} fusion(f32[640,3072]{1,0:T(8,128)} %get-tuple-element.71, f32[768,768]{1,0:T(8,128)} %get-tuple-element.123), kind=kOutput, calls=%fused_computation.95 | convolution fusion | flops 3019898880 | bytes 9764864 | tf_op jit(solution)/shard_map/jit(_solve_triangular)/triangular_solve | solution.py:81
  439.4 4.0 convolution_dynamic-update-slice_fusion
  443.4 4.2 slice_bitcast_fusion.6
  449.9 9.5 %pad_maximum_fusion.1 = (f32[2,768,768]{1,2,0:T(8,128)}, f32[2,768,768]{1,2,0:T(8,128)}, f32[2,768,768]{1,2,0:T(8,128)}) fusion(f32[1,768,768]{1,2,0:T(8,128)S(1)} %get-tuple-element.28, f32[1,768,768]{1,2,0:T(8,128)} %get-tuple-element.31, f32[1,768,768]{1,2,0:T(8,128)} %get-tuple-element.30, f32[1,768,768]{1,2,0:T(8,128)} %get-tuple-element.29), kind=kLoop, calls=%fused_computation.21 | loop fusion | flops 3538944 | bytes 23592960 | tf_op jit(solution)/shard_map/stack | solution.py:92
  461.5 7.4 collective-permute-start.4
  471.5 244.8 %collective-permute-done.5 = f32[768,768]{0,1:T(8,128)} collective-permute-done((f32[768,768]{0,1:T(8,128)}, f32[768,768]{0,1:T(8,128)}, u32[]{:S(2)}, u32[]{:S(2)}) %collective-permute-start.5) | collective-permute-done | bytes 2359328 | tf_op jit(solution)/shard_map/ppermute | solution.py:10
  716.3 9.5 %fusion.94 = f32[768,768]{1,0:T(8,128)} fusion(f32[768,768]{0,1:T(8,128)} %collective-permute-done.5), kind=kOutput, calls=%fused_computation.187 | convolution fusion | flops 5435817984 | bytes 4718592 | tf_op jit(solution)/shard_map/dot_general | solution.py:14
  725.8 4.2 fusion.92
  733.1 4.1 fusion.91
  743.5 5.3 maximum_bitcast_fusion
  748.8 9.6 %copy.45 = f32[1,4,768,768]{3,2,1,0:T(8,128)} copy(f32[1,4,768,768]{2,3,1,0:T(8,128)} %maximum_bitcast_fusion) | data formatting | bytes 18874368
  758.4 9.2 %fusion.18 = f32[768,768]{1,0:T(8,128)} fusion(f32[2,768,768]{1,2,0:T(8,128)} %collective-permute-done.2), kind=kOutput, calls=%fused_computation.30 | convolution fusion | flops 5435817984 | bytes 7077888 | tf_op jit(solution)/shard_map/dot_general | solution.py:14
  767.5 9.2 %fusion.20 = f32[768,768]{1,0:T(8,128)} fusion(f32[2,768,768]{1,2,0:T(8,128)} %collective-permute-done.3), kind=kOutput, calls=%fused_computation.34 | convolution fusion | flops 5435817984 | bytes 7077888 | tf_op jit(solution)/shard_map/dot_general | solution.py:14
  776.7 9.8 %fusion.19 = f32[768,768]{1,0:T(8,128)} fusion(f32[2,768,768]{1,2,0:T(8,128)} %collective-permute-done.4), kind=kOutput, calls=%fused_computation.32 | convolution fusion | flops 5435817984 | bytes 7077888 | tf_op jit(solution)/shard_map/dot_general | solution.py:14
  786.5 10.5 %fusion.25 = (f32[1,768,768]{2,1,0:T(8,128)}, f32[1,768,768]{2,1,0:T(8,128)}) fusion(f32[768,768]{1,0:T(8,128)} %copy.43, f32[768,768]{1,0:T(8,128)} %fusion.38, f32[768,768]{1,0:T(8,128)} %fusion.20, f32[]{:T(128)} %bitcast.29, pred[]{:T(512)S(6)} %gt.14, pred[]{:T(512)} %bitcast, f32[768,3072]{0,1:T(8,128)} %copy-done.5, f32[768,768]{1,0:T(8,128)} %copy.44, ...), kind=kLoop, calls=%fused_computation.43 | loop fusion | flops 5898240 | bytes 25952272 | tf_op jit(solution)/shard_map/stack | solution.py:117
  797.0 8.3 %fusion.79 = f32[768,768]{1,0:T(8,128)S(1)} fusion(f32[2,768,768]{1,2,0:T(8,128)} %collective-permute-done.3), kind=kOutput, calls=%fused_computation.169 | convolution fusion | flops 5435817984 | bytes 4718592 | tf_op jit(solution)/shard_map/dot_general | solution.py:14
  805.4 8.7 %fusion.21 = f32[768,768]{1,0:T(8,128)S(1)} fusion(f32[2,768,768]{1,2,0:T(8,128)} %collective-permute-done.4), kind=kOutput, calls=%fused_computation.37 | convolution fusion | flops 5435817984 | bytes 4718592 | tf_op jit(solution)/shard_map/dot_general | solution.py:14
  814.1 12.2 %select_bitcast_fusion = f32[1,768,768]{2,1,0:T(8,128)S(1)} fusion(f32[768,768]{1,0:T(8,128)S(1)} %fusion.79, f32[768,768]{1,0:T(8,128)S(1)} %fusion.21, f32[768,768]{1,0:T(8,128)S(1)} %copy-done.9, f32[768,768]{1,0:T(8,128)S(1)} %copy-done.3, f32[768,768]{1,0:T(8,128)S(1)} %get-tuple-element.41, f32[]{:T(128)} %bitcast.41, f32[]{:T(128)} %bitcast.25, ...), kind=kOutput, calls=%fused_computation.44 | convolution fusion | flops 5444665344 | bytes 16520705 | tf_op jit(solution)/shard_map/dot_general | solution.py:14
  (147 shorter events, 122.9 us)
Async XLA Ops:
  20.1 3.2 slice-start
  29.9 11.8 %copy-start.21 = (f32[1,768]{1,0:T(1,128)S(1)}, f32[1,768]{1,0:T(1,128)}, u32[]{:S(2)}) copy-start(f32[1,768]{1,0:T(1,128)} %param.6) | copy-start | bytes 9220
  29.9 68.0 %all-to-all-start = ((f32[128,2,4608]{2,1,0:T(2,128)}), f32[128,2,4608]{2,1,0:T(2,128)}, u32[]{:S(2)}, u32[]{:S(2)}) async-start(f32[128,2,4608]{2,1,0:T(2,128)} %maximum_maximum_fusion), calls=%async_computation | async-start | bytes 9437184 | tf_op jit(solution)/shard_map/all_to_all | solution.py:50
  104.5 9.9 %copy-start.4 = (f32[256,4608]{1,0:T(8,128)S(1)}, f32[256,4608]{1,0:T(8,128)}, u32[]{:S(2)}) copy-start(f32[256,4608]{1,0:T(8,128)} %all_to_all.7) | copy-start | bytes 14155780
  121.3 2.2 copy-start.2
  125.6 1.4 copy-start.20
  147.6 211.4 %collective-permute-start = (f32[768,768]{1,0:T(8,128)}, f32[768,768]{1,0:T(8,128)}, u32[]{:S(2)}, u32[]{:S(2)}) collective-permute-start(f32[768,768]{1,0:T(8,128)} %convolution_add_fusion), channel_id=1, source_target_pairs={{0,127},{1,0},{2,1},{3,2},{4,3},{5,4},{6,5},{7,6},{8,7},{9,8},{10,... | collective-permute-start | bytes 7077896 | tf_op jit(solution)/shard_map/ppermute | solution.py:10
  153.2 205.9 %collective-permute-start.1 = (f32[768,768]{1,0:T(8,128)}, f32[768,768]{1,0:T(8,128)}, u32[]{:S(2)}, u32[]{:S(2)}) collective-permute-start(f32[768,768]{1,0:T(8,128)} %fusion.38), channel_id=1, source_target_pairs={{0,126},{1,127},{2,0},{3,1},{4,2},{5,3},{6,4},{7,5},{8,6},{9,7},{1... | collective-permute-start | bytes 7077896 | tf_op jit(solution)/shard_map/ppermute | solution.py:10
  363.6 3.7 copy-start.1
  400.3 5.4 copy-start
  400.3 5.4 copy-start.6
  400.3 5.4 copy-start.8
  404.5 1.1 copy-start.19
  431.9 1.9 copy-start.14
  433.8 1.4 copy-start.15
  435.2 1.4 copy-start.16
  436.6 1.4 copy-start.18
  438.0 1.4 copy-start.17
  443.4 6.5 copy-start.5
  449.9 19.0 %copy-start.22 = (s32[128]{0:T(128)S(1)}, s32[128]{0:T(128)}, u32[]{:S(2)}) copy-start(s32[128]{0:T(128)} %param.7) | copy-start | bytes 1540
  459.4 266.4 %collective-permute-start.2 = (f32[2,768,768]{1,2,0:T(8,128)}, f32[2,768,768]{1,2,0:T(8,128)}, u32[]{:S(2)}, u32[]{:S(2)}) collective-permute-start(f32[2,768,768]{1,2,0:T(8,128)} %get-tuple-element.37), channel_id=1, source_target_pairs={{0,2},{1,3},{2,4},{3,5},{4,6},{5,7},{6,8},{7,9},{8,10},{9,11},{10,... | collective-permute-start | bytes 14155784 | tf_op jit(solution)/shard_map/ppermute | solution.py:10
  461.5 271.6 %collective-permute-start.3 = (f32[2,768,768]{1,2,0:T(8,128)}, f32[2,768,768]{1,2,0:T(8,128)}, u32[]{:S(2)}, u32[]{:S(2)}) collective-permute-start(f32[2,768,768]{1,2,0:T(8,128)} %get-tuple-element.38), channel_id=1, source_target_pairs={{0,1},{1,2},{2,3},{3,4},{4,5},{5,6},{6,7},{7,8},{8,9},{9,10},{10,1... | collective-permute-start | bytes 14155784 | tf_op jit(solution)/shard_map/ppermute | solution.py:10
  461.5 278.9 %collective-permute-start.4 = (f32[2,768,768]{1,2,0:T(8,128)}, f32[2,768,768]{1,2,0:T(8,128)}, u32[]{:S(2)}, u32[]{:S(2)}) collective-permute-start(f32[2,768,768]{1,2,0:T(8,128)} %get-tuple-element.39), channel_id=1, source_target_pairs={{0,127},{1,0},{2,1},{3,2},{4,3},{5,4},{6,5},{7,6},{8,7},{9,8},{10,... | collective-permute-start | bytes 14155784 | tf_op jit(solution)/shard_map/ppermute | solution.py:10
  468.9 247.4 %collective-permute-start.5 = (f32[768,768]{0,1:T(8,128)}, f32[768,768]{0,1:T(8,128)}, u32[]{:S(2)}, u32[]{:S(2)}) collective-permute-start(f32[768,768]{0,1:T(8,128)} %get-tuple-element.32), channel_id=1, source_target_pairs={{0,126},{1,127},{2,0},{3,1},{4,2},{5,3},{6,4},{7,5},{8,6},{9,7},{1... | collective-permute-start | bytes 7077896 | tf_op jit(solution)/shard_map/ppermute | solution.py:10
  740.4 2.4 copy-start.10
  740.4 3.1 copy-start.11
  776.7 9.8 %copy-start.7 = (f32[768,768]{1,0:T(8,128)S(1)}, f32[768,768]{1,0:T(8,128)}, u32[]{:S(2)}) copy-start(f32[768,768]{1,0:T(8,128)} %convolution_add_fusion) | copy-start | bytes 7077892
  805.3 8.7 %copy-start.3 = (f32[768,768]{1,0:T(8,128)S(1)}, f32[768,768]{1,0:T(8,128)}, u32[]{:S(2)}) copy-start(f32[768,768]{1,0:T(8,128)} %copy-done.2) | copy-start | bytes 7077892
  805.4 8.7 %copy-start.9 = (f32[768,768]{1,0:T(8,128)S(1)}, f32[768,768]{1,0:T(8,128)}, u32[]{:S(2)}) copy-start(f32[768,768]{1,0:T(8,128)} %fusion.94) | copy-start | bytes 7077892
  814.1 12.2 %copy-start.12 = (f32[1,768,768]{2,1,0:T(8,128)S(1)}, f32[1,768,768]{2,1,0:T(8,128)}, u32[]{:S(2)}) copy-start(f32[1,768,768]{2,1,0:T(8,128)} %get-tuple-element.26) | copy-start | bytes 7077892
  814.1 12.2 %copy-start.13 = (f32[1,768,768]{2,1,0:T(8,128)S(1)}, f32[1,768,768]{2,1,0:T(8,128)}, u32[]{:S(2)}) copy-start(f32[1,768,768]{2,1,0:T(8,128)} %get-tuple-element.27) | copy-start | bytes 7077892
where the time goes:
time: 839 us; the launch traced here: 830 us
  waiting for transfers between devices  301 us (36%)
  other arithmetic  231 us (28%)
  matrix products  151 us (18%)
  local copies, waits for them, and re-layouts  113 us (13%)
  starting transfers between devices  25.6 us (3%)
    ppermute x6, waiting for transfers between devices, passed_along(): return lax.ppermute(value, axis, pairs)  245 us
    another operation x22, other arithmetic, local(): factor = jnp.linalg.cholesky(diag_tile)  124 us
    dot_general x13, matrix products, gram_product(): lax.dot_general(left_op, right_op, (((0,), (0,)), ((), ())), precision=la...  89.4 us
    another operation x3, other arithmetic, local(): solved = jax.scipy.linalg.solve_triangular(factor, right_sides, lower=True)  60.6 us
    all_to_all x1, waiting for transfers between devices, local(): lax.all_to_all(payload.reshape(block_count * capacity, lane_count), ('gx'...  56.1 us
    another operation x11, matrix products, local(): solved = jax.scipy.linalg.solve_triangular(factor, right_sides, lower=True)  52.1 us
    unnamed x54, local copies, waits for them, and re-layouts  28.8 us
    another operation x18, local copies, waits for them, and re-layouts  17.6 us
  transfers between devices with their start and end apart: 7, of which 2 were waited for; matrix products, arithmetic and copies ran while one was open for 27% of the time, Pallas kernels for 0%

commit v1 on v0

v1 whole, which is shorter than its diff:
```python
import jax
import jax.numpy as jnp
from jax import lax
from jax.experimental import pallas as pl
from jax.experimental.pallas import tpu as pltpu
from jax.sharding import PartitionSpec as P

F32 = jnp.float32
BF16 = jnp.bfloat16
AXES = ("gx", "gy")


def split2(x):
    hi = x.astype(BF16)
    lo = (x - hi.astype(F32)).astype(BF16)
    return hi, lo


def dg(x, y, dims=((1,), (0,))):
    return lax.dot_general(x, y, (dims, ((), ())), preferred_element_type=F32)


def dot3(x, y, dims=((1,), (0,))):
    return dg(x[0], y[0], dims) + (dg(x[0], y[1], dims) + dg(x[1], y[0], dims))


def bucket_kernel(strips_ref, col_ref, row_ref, flag_ref, first_ref, second_ref):
    n = row_ref.shape[1]
    width = strips_ref.shape[1] // 3
    row = row_ref[...]
    col = col_ref[...]
    r_id = lax.broadcasted_iota(jnp.int32, (n, n), 0)
    c_id = lax.broadcasted_iota(jnp.int32, (n, n), 1)
    same = jnp.where((col == row) & (r_id < c_id), 1, 0)
    within = jnp.sum(same, axis=0, keepdims=True)
    t_id = lax.broadcasted_iota(jnp.int32, (2 * n, n), 0)
    lane = lax.broadcasted_iota(jnp.int32, (2 * n, n), 1)
    block = t_id >> 1
    slot_ok = within == (t_id & 1)
    hit = [slot_ok & (((row + shift) & (n - 1)) == block) for shift in range(4)]
    flags = flag_ref[...]

    def flag_before(step):
        chosen = lane == ((block + (n - step)) & (n - 1))
        return jnp.sum(jnp.where(chosen, flags, 0), axis=1, keepdims=True) > 0

    one_before = flag_before(1)
    two_before = flag_before(2)

    def mask(cond):
        return jnp.where(cond, 1.0, 0.0).astype(BF16)

    pieces = []
    for i in range(3):
        x = strips_ref[:, i * width : (i + 1) * width]
        hi = x.astype(BF16)
        rest = x - hi.astype(F32)
        mid = rest.astype(BF16)
        low = (rest - mid.astype(F32)).astype(BF16)
        pieces.append((hi, mid, low))

    def pick(select, i):
        hi, mid, low = pieces[i]
        return dg(select, hi) + (dg(select, mid) + dg(select, low))

    for i in range(3):
        first_ref[:, i * width : (i + 1) * width] = pick(mask(hit[i]), i)
    second_ref[:, 0:width] = pick(mask(hit[1] & ~one_before), 0) + pick(
        mask(hit[3] & one_before), 1
    )
    second_ref[:, width : 2 * width] = pick(mask(hit[2]), 1)
    second_ref[:, 2 * width : 3 * width] = pick(mask(hit[2] & ~two_before), 0) + pick(
        mask(hit[3] & two_before), 2
    )


def bucket(strips, index, flags):
    n = strips.shape[0]
    wide = strips.shape[1] * strips.shape[2]
    shape = jax.ShapeDtypeStruct((2 * n, wide), F32)
    return pl.pallas_call(
        bucket_kernel,
        out_shape=(shape, shape),
        name="bucket",
    )(strips.reshape(n, wide), index, index.reshape(1, n), flags.reshape(1, n))


def chol_block(a):
    n = a.shape[0]
    groups = n // 8
    sub = lax.broadcasted_iota(jnp.int32, (8, n), 0)
    lane = lax.broadcasted_iota(jnp.int32, (8, n), 1)
    left = [a[8 * v : 8 * v + 8, :] for v in range(groups)]
    right = [jnp.where(lane == sub + 8 * v, 1.0, 0.0).astype(F32) for v in range(groups)]

    def lanes_of(x, k):
        return [jnp.broadcast_to(x[:, 8 * k + i : 8 * k + i + 1], (8, n)) for i in range(8)]

    def sub_of(x, i):
        return jnp.broadcast_to(x[i : i + 1, :], (8, n))

    for k in range(groups):
        c = lanes_of(left[k], k)
        u, v_in = left[k], right[k]
        scale, row_u, row_v, row_c = [], [], [], []
        for i in range(8):
            inv = lax.rsqrt(sub_of(c[i], i))
            ru = sub_of(u, i) * inv
            rv = sub_of(v_in, i) * inv
            rc = [None] * 8
            m = jnp.where(sub > i, c[i] * inv, 0.0)
            for j in range(i + 1, 8):
                rc[j] = sub_of(c[j], i) * inv
                c[j] = c[j] - m * rc[j]
            u = jnp.where(sub == i, ru, u - m * ru)
            v_in = jnp.where(sub == i, rv, v_in - m * rv)
            scale.append(inv)
            row_u.append(ru)
            row_v.append(rv)
            row_c.append(rc)
        left[k], right[k] = u, v_in
        for g in range(k + 1, groups):
            c = lanes_of(left[g], k)
            x, y = left[g], right[g]
            for i in range(8):
                m = c[i] * scale[i]
                for j in range(i + 1, 8):
                    c[j] = c[j] - m * row_c[i][j]
                x = x - m * row_u[i]
                y = y - m * row_v[i]
            left[g], right[g] = x, y
    upper = jnp.concatenate(left, axis=0)
    r_id = lax.broadcasted_iota(jnp.int32, (n, n), 0)
    c_id = lax.broadcasted_iota(jnp.int32, (n, n), 1)
    return jnp.where(c_id >= r_id, upper, 0.0), jnp.concatenate(right, axis=0)


def chol_kernel(recv_ref, shift_ref, l_ref, w0_ref, w1_ref, w2_ref, ath_ref, atl_ref, m_ref, x_ref):
    size = shift_ref.shape[1]
    slots = recv_ref.shape[0]
    nb = 128
    count = size // nb
    w_refs = (w0_ref, w1_ref, w2_ref)
    l_ref[...] = jnp.zeros_like(l_ref)
    parts = []
    for i in range(3):
        at = recv_ref[:, i * size : (i + 1) * size].T
        m_ref[:, size + i * slots : size + (i + 1) * slots] = at
        hi, lo = split2(at)
        ath_ref[:, i * slots : (i + 1) * slots] = hi
        atl_ref[:, i * slots : (i + 1) * slots] = lo
    for blk in range(0, size, 256):
        total = None
        for i in range(3):
            a = split2(recv_ref[:, i * size + blk : i * size + blk + 256])
            t = (ath_ref[:, i * slots : (i + 1) * slots], atl_ref[:, i * slots : (i + 1) * slots])
            add = dot3(t, a)
            total = add if total is None else total + add
        r_id = lax.broadcasted_iota(jnp.int32, (size, 256), 0)
        c_id = lax.broadcasted_iota(jnp.int32, (size, 256), 1) + blk
        m_ref[:, blk : blk + 256] = total + jnp.where(
            r_id == c_id, shift_ref[:, blk : blk + 256], 0.0
        )

    def step(k, carry):
        at = pl.multiple_of(k * nb, nb)
        upper, inverse = chol_block(m_ref[pl.ds(at, nb), pl.ds(at, nb)])
        l_ref[pl.ds(at, nb), pl.ds(at, nb)] = upper.T
        inv = split2(inverse)
        for blk in range(0, 2 * size, 256):
            x_ref[:, blk : blk + 256] = dot3(inv, split2(m_ref[pl.ds(at, nb), blk : blk + 256]))
        for i in range(3):
            w_refs[i][pl.ds(at, nb), :] = x_ref[:, size + i * slots : size + (i + 1) * slots]

        def trail(r, inner):
            to = pl.multiple_of(r * nb, nb)
            low = x_ref[:, pl.ds(to, nb)].T
            l_ref[pl.ds(to, nb), pl.ds(at, nb)] = low
            low = split2(low)
            for blk in range(0, 2 * size, 256):
                m_ref[pl.ds(to, nb), blk : blk + 256] -= dot3(
                    low, split2(x_ref[:, blk : blk + 256])
                )
            return inner

        return lax.fori_loop(k + 1, count, trail, carry)

    lax.fori_loop(0, count, step, 0)


def chol(recv, shift):
    size = shift.shape[1]
    slots = recv.shape[0]
    w = jax.ShapeDtypeStruct((size, slots), F32)
    half = jax.ShapeDtypeStruct((size, 3 * slots), BF16)
    return pl.pallas_call(
        chol_kernel,
        out_shape=(jax.ShapeDtypeStruct((size, size), F32), w, w, w, half, half),
        scratch_shapes=[pltpu.VMEM((size, size + 3 * slots), F32), pltpu.VMEM((128, size + 3 * slots), F32)],
        compiler_params=pltpu.CompilerParams(vmem_limit_bytes=50 * 2**20),
        name="chol",
    )(recv, shift)


def last_kernel(
    flag_ref, recv_ref, ath_ref, atl_ref, q_ref, shift_ref, l_ref, w1_ref, w2_ref,
    m1w0_ref, m1w1_ref, m2w0_ref, p1w1_ref, p1w2_ref, p2w2_ref, e_ref,
    schur_ref, coup_ref,
    qh_ref, ql_ref, wh_ref, wl_ref, wth_ref, wtl_ref, f_ref,
):
    step = pl.program_id(0)
    size = shift_ref.shape[1]
    slots = recv_ref.shape[0]
    cols = schur_ref.shape[3]
    fm2, fm1, own, fp1, fp2 = [flag_ref[i] > 0 for i in range(5)]
    w_refs = (m1w0_ref, m1w1_ref, m2w0_ref, p1w1_ref, p1w2_ref, p2w2_ref)

    @pl.when(step == 0)
    def _():
        for i in range(3):
            hi, lo = split2(q_ref[:, i * size : (i + 1) * size].T)
            qh_ref[:, i * slots : (i + 1) * slots] = hi
            ql_ref[:, i * slots : (i + 1) * slots] = lo
        for i in range(6):
            hi, lo = split2(w_refs[i][...])
            wh_ref[i] = hi
            wl_ref[i] = lo
        for i in range(7):
            hi, lo = split2((w_refs[i] if i < 6 else e_ref)[...].T)
            wth_ref[i] = hi
            wtl_ref[i] = lo

    base = pl.multiple_of(step * cols, cols)

    def a_part(i):
        return recv_ref[:, pl.ds(pl.multiple_of(i * size + base, cols), cols)]

    def w_of(i):
        return wh_ref[i], wl_ref[i]

    def wt_of(i):
        return wth_ref[i], wtl_ref[i]

    def at_of(i):
        return ath_ref[:, i * slots : (i + 1) * slots], atl_ref[:, i * slots : (i + 1) * slots]

    def q_of(i):
        return qh_ref[:, i * slots : (i + 1) * slots], ql_ref[:, i * slots : (i + 1) * slots]

    a0, a1, a2 = [split2(a_part(i)) for i in range(3)]
    coup_ref[0, 0] = dot3(w_of(5), a0)
    coup_ref[0, 1] = dot3(w_of(3), a0) + dot3(w_of(4), a1)
    coup_ref[0, 2] = dot3(w_of(0), a1) + dot3(w_of(1), a2)
    coup_ref[0, 3] = dot3(w_of(2), a2)

    @pl.when(own)
    def _():
        w1 = split2(w1_ref[pl.ds(base, cols), :])
        w2 = split2(w2_ref[pl.ds(base, cols), :])
        over = ((1,), (1,))
        schur_ref[0, 0] = dot3(q_of(2), w2, over)
        schur_ref[0, 1] = dot3(q_of(0), w1, over) + dot3(q_of(1), w2, over)
        schur_ref[0, 2] = l_ref[:, pl.ds(base, cols)]

    @pl.when(jnp.logical_not(own))
    def _():
        f_ref[...] = jnp.zeros_like(f_ref)

        @pl.when(fp2)
        def _():
            f_ref[0] = dot3(wt_of(5), split2(coup_ref[0, 0]))

        @pl.when(fp1)
        def _():
            c = split2(coup_ref[0, 1])
            f_ref[0] += dot3(wt_of(3), c)
            f_ref[1] = dot3(wt_of(4), c)

        @pl.when(fm1)
        def _():
            c = split2(coup_ref[0, 2])
            f_ref[1] += dot3(wt_of(0), c)
            f_ref[2] = dot3(wt_of(1), c)
            f_ref[3] = dot3(wt_of(6), c)

        @pl.when(fm2)
        def _():
            c = split2(coup_ref[0, 3])
            f_ref[2] += dot3(wt_of(2), c)
            f_ref[3] = dot3(wt_of(6), c)

        y = [split2(a_part(i) - f_ref[i]) for i in range(3)]
        r_id = lax.broadcasted_iota(jnp.int32, (size, cols), 0)
        c_id = lax.broadcasted_iota(jnp.int32, (size, cols), 1) + base
        diag = jnp.where(r_id == c_id, shift_ref[:, pl.ds(base, cols)], 0.0)
        schur_ref[0, 2] = (
            dot3(at_of(0), y[0]) + dot3(at_of(1), y[1]) + dot3(at_of(2), y[2])
        ) + diag

        @pl.when(fm1)
        def _():
            schur_ref[0, 1] = coup_ref[0, 2]

        @pl.when(jnp.logical_not(fm1))
        def _():
            schur_ref[0, 1] = dot3(q_of(0), y[1]) + dot3(q_of(1), y[2])

            @pl.when(fm2)
            def _():
                schur_ref[0, 1] -= dot3(q_of(2), split2(f_ref[3]))

        @pl.when(fm2)
        def _():
            schur_ref[0, 0] = coup_ref[0, 3]

        @pl.when(jnp.logical_not(fm2))
        def _():
            schur_ref[0, 0] = dot3(q_of(2), y[2])

            @pl.when(fm1)
            def _():
                schur_ref[0, 0] -= dot3(q_of(0), split2(f_ref[3]))


def last(flags, recv, ath, atl, q, shift, l, w1, w2, others):
    size = shift.shape[1]
    slots = recv.shape[0]
    cols = 256
    whole = pl.BlockSpec(memory_space=pltpu.VMEM)
    return pl.pallas_call(
        last_kernel,
        grid=(size // cols,),
        in_specs=[pl.BlockSpec(memory_space=pltpu.SMEM)] + [whole] * 15,
        out_specs=(
            pl.BlockSpec((1, 3, size, cols), lambda n: (0, 0, 0, n)),
            pl.BlockSpec((1, 4, size, cols), lambda n: (0, 0, 0, n)),
        ),
        out_shape=(
            jax.ShapeDtypeStruct((1, 3, size, size), F32),
            jax.ShapeDtypeStruct((1, 4, size, size), F32),
        ),
        scratch_shapes=[
            pltpu.VMEM((size, 3 * slots), BF16),
            pltpu.VMEM((size, 3 * slots), BF16),
            pltpu.VMEM((6, size, slots), BF16),
            pltpu.VMEM((6, size, slots), BF16),
            pltpu.VMEM((7, slots, size), BF16),
            pltpu.VMEM((7, slots, size), BF16),
            pltpu.VMEM((4, slots, cols), F32),
        ],
        compiler_params=pltpu.CompilerParams(vmem_limit_bytes=62 * 2**20),
        name="last",
    )(flags, recv, ath, atl, q, shift, l, w1, w2, *others)


def passed_along(value, steps):
    count = lax.axis_size(AXES)
    pairs = [(source, (source + steps) % count) for source in range(count)]
    return lax.ppermute(value, AXES, pairs)


def exchange(payload):
    count = lax.axis_size(AXES)
    wide = payload.shape[1]
    got = lax.all_to_all(
        payload.reshape(count, -1, wide), AXES, split_axis=0, concat_axis=0, tiled=True
    )
    return got.reshape(payload.shape)


def local(strips, index, shift, flags):
    count = lax.axis_size(AXES)
    own = lax.axis_index(AXES)
    first, second = bucket(strips, index, flags)
    recv = exchange(first)
    l, w0, w1, w2, ath, atl = chol(recv, shift)
    q = exchange(second)
    near = jnp.take(flags, (own + jnp.arange(-2, 3)) % count)
    m1w0 = passed_along(w0, 1)
    m1w1 = passed_along(w1, 1)
    p1w2 = passed_along(w2, -1)
    p1w1 = passed_along(w1, -1)
    m2w0 = passed_along(m1w0, 1)
    p2w2 = passed_along(p1w2, -1)
    e = passed_along(jnp.where(near[2] > 0, w2, m1w1), 1)
    others = (m1w0, m1w1, m2w0, p1w1, p1w2, p2w2, e)
    return last(near, recv, ath, atl, q, shift, l, w1, w2, others)


def solution(mesh):
    in_specs = (P(AXES, None, None), P(AXES, None), P(AXES, None), P())
    out_specs = (P(AXES, None, None, None), P(AXES, None, None, None))
    return jax.shard_map(local, mesh=mesh, in_specs=in_specs, out_specs=out_specs, check_vma=False)
```

time: 839 us -> 215 us (0.26); the launches traced: 830 us -> 215 us
  other arithmetic: 231 us -> 1.15 us
  waiting for transfers between devices: 301 us -> 81.3 us
  matrix products: 151 us -> 0 us
  local copies, waits for them, and re-layouts: 113 us -> 21.7 us
  Pallas kernels: 0 us -> 76.2 us
    another operation x28 -> x0, other arithmetic: 204 us -> none  [the longest x22 124 us: local(): factor = jnp.linalg.cholesky(diag_tile)]
    ppermute x6 -> x7, waiting for transfers between devices: 245 us -> 52.7 us  [passed_along(): return lax.ppermute(value, AXES, pairs)]
    dot_general x13 -> x0, matrix products: 89.4 us -> none  [gram_product(): lax.dot_general(left_op, right_op, (((0,), (0,)), ((), ())), precision=la...]
    pallas_call x0 -> x3, Pallas kernels: none -> 76.2 us  [the longest x1 41.9 us: chol(): pl.pallas_call(chol_kernel, out_shape=(jax.ShapeDtypeStruct((size, size),...]
    another operation x21 -> x0, matrix products: 61.9 us -> none  [the longest x11 52.1 us: local(): solved = jax.scipy.linalg.solve_triangular(factor, right_sides, lower=True)]
    another operation x31 -> x0, local copies, waits for them, and re-layouts: 37.2 us -> none
    all_to_all x1 -> x2, waiting for transfers between devices: 56.1 us -> 28.6 us  [exchange(): lax.all_to_all(payload.reshape(count, -1, wide), AXES, split_axis=0, conc...]
    unnamed x54 -> x18, local copies, waits for them, and re-layouts: 28.8 us -> 4.96 us
  transfers between devices with their start and end apart: 7 -> 9, of which waited for: 2 -> 4; matrix products, arithmetic and copies ran while one was open for 27% -> 6% of each run, Pallas kernels for 0% -> 19%
where the time goes in v1:
time: 215 us
  waiting for transfers between devices  81.3 us (38%)
  Pallas kernels  76.2 us (35%)
  starting transfers between devices  33 us (15%)
  local copies, waits for them, and re-layouts  21.7 us (10%)
    ppermute x7, waiting for transfers between devices, passed_along(): return lax.ppermute(value, AXES, pairs)  52.7 us
    pallas_call x1, Pallas kernels, chol(): pl.pallas_call(chol_kernel, out_shape=(jax.ShapeDtypeStruct((size, size),...  41.9 us
    pallas_call x1, Pallas kernels, last(): pl.pallas_call(last_kernel, grid=(size // cols,), in_specs=[pl.BlockSpec(...  28.9 us
    all_to_all x2, waiting for transfers between devices, exchange(): lax.all_to_all(payload.reshape(count, -1, wide), AXES, split_axis=0, conc...  28.6 us
    all_to_all x2, starting transfers between devices, exchange(): lax.all_to_all(payload.reshape(count, -1, wide), AXES, split_axis=0, conc...  17.1 us
    ppermute x7, starting transfers between devices, passed_along(): return lax.ppermute(value, AXES, pairs)  15.9 us
    reshape x2, local copies, waits for them, and re-layouts, exchange(): payload.reshape(count, -1, wide)  7.53 us
    reshape x2, local copies, waits for them, and re-layouts, exchange(): return got.reshape(payload.shape)  6.59 us
  transfers between devices with their start and end apart: 9, of which 4 were waited for; matrix products, arithmetic and copies ran while one was open for 6% of the time, Pallas kernels for 19%

profile of v1, /device:TPU:0, one launch (start us, length us, event | category | flops | bytes accessed | tf_op | source)
XLA Modules:
  0.0 214.8 jit_solution(7774754935129087423)
XLA Ops:
  0.6 1.4 copy.10.col_ref
  2.0 1.6 copy.8
  3.7 1.4 copy.9.strips_ref
  5.1 5.4 %bucket.1 = (f32[256,2304]{1,0:T(8,128)}, f32[256,2304]{1,0:T(8,128)}) custom-call(f32[128,2304]{1,0:T(8,128)} %copy.9.strips_ref, s32[128,1]{1,0:T(8,128)} %copy.10.col_ref, s32[1,128]{1,0:T(1,128)} %bitcast.8, s32[1,128]{1,0:T(1,128)} %bitcast.6), custom_call_target="tpu_custom_call" | custom-call | tf_op jit(solution)/shard_map/bucket/pallas_call | solution.py:81
  10.5 3.8 %reshape.87 = f32[128,2,2304]{2,1,0:T(2,128)} reshape(f32[256,2304]{1,0:T(8,128)} %get-tuple-element.10) | data formatting | bytes 4718592 | tf_op jit(solution)/shard_map/reshape | solution.py:366
  14.3 11.2 %all-to-all-start = ((f32[128,2,2304]{2,1,0:T(2,128)}), f32[128,2,2304]{2,1,0:T(2,128)S(1)}, u32[]{:S(2)}, u32[]{:S(2)}) async-start(f32[128,2,2304]{2,1,0:T(2,128)} %reshape.87), calls=%async_computation | async-start | bytes 4718592 | tf_op jit(solution)/shard_map/all_to_all | solution.py:365
  25.5 3.8 %reshape.89 = f32[128,2,2304]{2,1,0:T(2,128)} reshape(f32[256,2304]{1,0:T(8,128)} %get-tuple-element.13) | data formatting | bytes 4718592 | tf_op jit(solution)/shard_map/reshape | solution.py:366
  29.2 28.6 %all-to-all-done = f32[128,2,2304]{2,1,0:T(2,128)S(1)} async-done(((f32[128,2,2304]{2,1,0:T(2,128)}), f32[128,2,2304]{2,1,0:T(2,128)S(1)}, u32[]{:S(2)}, u32[]{:S(2)}) %all-to-all-start) | async-done | bytes 2359328 | tf_op jit(solution)/shard_map/all_to_all | solution.py:365
  57.9 5.9 %all-to-all-start.1 = ((f32[128,2,2304]{2,1,0:T(2,128)}), f32[128,2,2304]{2,1,0:T(2,128)}, u32[]{:S(2)}, u32[]{:S(2)}) async-start(f32[128,2,2304]{2,1,0:T(2,128)} %reshape.89), calls=%async_computation.1 | async-start | bytes 4718592 | tf_op jit(solution)/shard_map/all_to_all | solution.py:365
  63.8 0.0 copy-start.3
  63.8 2.6 %reshape.88.recv_ref = f32[256,2304]{1,0:T(8,128)} reshape(f32[128,2,2304]{2,1,0:T(2,128)S(1)} %all-to-all-done) | data formatting | bytes 4718592 | tf_op jit(solution)/shard_map/reshape | solution.py:368
  66.4 0.0 copy-done.3
  66.4 0.0 copy-start.4
  66.4 41.9 %chol.1 = (f32[768,768]{1,0:T(8,128)}, f32[768,256]{1,0:T(8,128)S(1)}, f32[768,256]{1,0:T(8,128)S(1)}, f32[768,256]{1,0:T(8,128)S(1)}, bf16[768,768]{1,0:T(8,128)(2,1)S(1)}, /*index=5*/bf16[768,768]{1,0:T(8,128)(2,1)}) custom-call(f32[256,2304]{1,0:T(8,128)} %reshape.88.recv_ref, f32[1,768]{1,0:T(1,128)S(1)} %copy-done.3), custom_call_target="tpu_custom_call" | custom-call | tf_op jit(solution)/shard_map/chol/pallas_call | solution.py:196
  108.3 0.0 copy-start.1
  108.3 1.0 copy-done.1
  109.3 0.0 copy-start
  109.3 0.0 copy-start.2
  109.3 0.6 collective-permute-start.1
  109.9 1.5 collective-permute-start
  111.4 5.7 %collective-permute-start.4 = (f32[768,256]{1,0:T(8,128)S(1)}, f32[768,256]{1,0:T(8,128)}, u32[]{:S(2)}, u32[]{:S(2)}) collective-permute-start(f32[768,256]{1,0:T(8,128)S(1)} %get-tuple-element.16.w2_ref), channel_id=1, source_target_pairs={{0,127},{1,0},{2,1},{3,2},{4,3},{5,4},{6,5},{7,6},{8,7},{9,8},{10,... | collective-permute-start | bytes 2359304 | tf_op jit(solution)/shard_map/ppermute | solution.py:359
  117.1 0.0 copy-done.4
  117.2 0.6 gather_fusion
  117.8 0.0 copy-start.7
  117.8 0.6 slice.3
  119.1 0.9 collective-permute-start.3
  120.0 14.5 %collective-permute-done.1.m1w1_ref = f32[768,256]{1,0:T(8,128)S(1)} collective-permute-done((f32[768,256]{1,0:T(8,128)S(1)}, f32[768,256]{1,0:T(8,128)S(1)}, u32[]{:S(2)}, u32[]{:S(2)}) %collective-permute-start.1) | collective-permute-done | bytes 786464 | tf_op jit(solution)/shard_map/ppermute | solution.py:359
  134.5 0.0 copy-start.5
  134.5 1.1 broadcast_select_fusion
  135.6 0.0 collective-permute-start.6
  135.6 15.8 %collective-permute-done.m1w0_ref = f32[768,256]{1,0:T(8,128)} collective-permute-done((f32[768,256]{1,0:T(8,128)S(1)}, f32[768,256]{1,0:T(8,128)}, u32[]{:S(2)}, u32[]{:S(2)}) %collective-permute-start) | collective-permute-done | bytes 786464 | tf_op jit(solution)/shard_map/ppermute | solution.py:359
  151.5 0.0 collective-permute-start.2
  151.5 0.0 collective-permute-done.4.p1w2_ref
  151.5 7.2 %collective-permute-start.5 = (f32[768,256]{1,0:T(8,128)}, f32[768,256]{1,0:T(8,128)}, u32[]{:S(2)}, u32[]{:S(2)}) collective-permute-start(f32[768,256]{1,0:T(8,128)} %collective-permute-done.4.p1w2_ref), channel_id=1, source_target_pairs={{0,127},{1,0},{2,1},{3,2},{4,3},{5,4},{6,5},{7,6},{8,7},{9,8},{10,... | collective-permute-start | bytes 2359304 | tf_op jit(solution)/shard_map/ppermute | solution.py:359
  158.7 0.0 all-to-all-done.1
  158.7 3.9 %reshape.90.q_ref = f32[256,2304]{1,0:T(8,128)} reshape(f32[128,2,2304]{2,1,0:T(2,128)} %all-to-all-done.1) | data formatting | bytes 4718592 | tf_op jit(solution)/shard_map/reshape | solution.py:368
  162.6 0.0 copy-done
  162.6 0.0 copy-done.2
  162.6 0.0 copy-done.7
  162.6 0.0 copy-done.5
  162.6 0.0 collective-permute-done.3.p1w1_ref
  162.6 22.3 %collective-permute-done.2.m2w0_ref = f32[768,256]{1,0:T(8,128)S(1)} collective-permute-done((f32[768,256]{1,0:T(8,128)}, f32[768,256]{1,0:T(8,128)S(1)}, u32[]{:S(2)}, u32[]{:S(2)}) %collective-permute-start.2) | collective-permute-done | bytes 786464 | tf_op jit(solution)/shard_map/ppermute | solution.py:359
  185.0 0.0 copy-start.6
  185.0 0.0 collective-permute-done.6.e_ref
  185.0 0.0 collective-permute-done.5.p2w2_ref
  185.0 0.9 copy-done.6
  185.9 28.9 %last.1 = (f32[1,3,768,768]{3,2,1,0:T(8,128)}, f32[1,4,768,768]{3,2,1,0:T(8,128)}) custom-call(s32[5]{0:T(128)} %copy-done.7, f32[256,2304]{1,0:T(8,128)} %reshape.88.recv_ref, bf16[768,768]{1,0:T(8,128)(2,1)} %copy-done.1, bf16[768,768]{1,0:T(8,128)(2,1)} %get-tuple-element.12.atl_ref, f32[256,2304]{1,0:T(8,128)} %reshape.90.q_ref, f32[1,768]{1,0:T(1,128)} %shift_ref.3, ...), custom_call_target="tpu_custom_call" | custom-call | tf_op jit(solution)/shard_map/last/pallas_call | solution.py:330
  (3 shorter events, 0.0 us)
Async XLA Ops:
  14.3 43.6 %all-to-all-start = ((f32[128,2,2304]{2,1,0:T(2,128)}), f32[128,2,2304]{2,1,0:T(2,128)S(1)}, u32[]{:S(2)}, u32[]{:S(2)}) async-start(f32[128,2,2304]{2,1,0:T(2,128)} %reshape.87), calls=%async_computation | async-start | bytes 4718592 | tf_op jit(solution)/shard_map/all_to_all | solution.py:365
  57.9 100.8 %all-to-all-start.1 = ((f32[128,2,2304]{2,1,0:T(2,128)}), f32[128,2,2304]{2,1,0:T(2,128)}, u32[]{:S(2)}, u32[]{:S(2)}) async-start(f32[128,2,2304]{2,1,0:T(2,128)} %reshape.89), calls=%async_computation.1 | async-start | bytes 4718592 | tf_op jit(solution)/shard_map/all_to_all | solution.py:365
  63.8 2.7 %copy-start.3 = (f32[1,768]{1,0:T(1,128)S(1)}, f32[1,768]{1,0:T(1,128)}, u32[]{:S(2)}) copy-start(f32[1,768]{1,0:T(1,128)} %shift_ref.3) | copy-start | bytes 9220
  66.4 50.7 %copy-start.4 = (s32[128]{0:T(128)S(1)}, s32[128]{0:T(128)}, u32[]{:S(2)}) copy-start(s32[128]{0:T(128)} %param.7) | copy-start | bytes 1540
  108.3 1.0 copy-start.1
  109.3 53.3 %copy-start = (f32[768,256]{1,0:T(8,128)}, f32[768,256]{1,0:T(8,128)S(1)}, u32[]{:S(2)}) copy-start(f32[768,256]{1,0:T(8,128)S(1)} %get-tuple-element.16.w2_ref) | copy-start | bytes 2359300
  109.3 53.3 %copy-start.2 = (f32[768,256]{1,0:T(8,128)}, f32[768,256]{1,0:T(8,128)S(1)}, u32[]{:S(2)}) copy-start(f32[768,256]{1,0:T(8,128)S(1)} %get-tuple-element.15.w1_ref) | copy-start | bytes 2359300
  109.3 25.2 %collective-permute-start.1 = (f32[768,256]{1,0:T(8,128)S(1)}, f32[768,256]{1,0:T(8,128)S(1)}, u32[]{:S(2)}, u32[]{:S(2)}) collective-permute-start(f32[768,256]{1,0:T(8,128)S(1)} %get-tuple-element.15.w1_ref), channel_id=1, source_target_pairs={{0,1},{1,2},{2,3},{3,4},{4,5},{5,6},{6,7},{7,8},{8,9},{9,10},{10,1... | collective-permute-start | bytes 2359304 | tf_op jit(solution)/shard_map/ppermute | solution.py:359
  109.9 41.5 %collective-permute-start = (f32[768,256]{1,0:T(8,128)S(1)}, f32[768,256]{1,0:T(8,128)}, u32[]{:S(2)}, u32[]{:S(2)}) collective-permute-start(f32[768,256]{1,0:T(8,128)S(1)} %get-tuple-element.17), channel_id=1, source_target_pairs={{0,1},{1,2},{2,3},{3,4},{4,5},{5,6},{6,7},{7,8},{8,9},{9,10},{10,1... | collective-permute-start | bytes 2359304 | tf_op jit(solution)/shard_map/ppermute | solution.py:359
  111.4 40.1 %collective-permute-start.4 = (f32[768,256]{1,0:T(8,128)S(1)}, f32[768,256]{1,0:T(8,128)}, u32[]{:S(2)}, u32[]{:S(2)}) collective-permute-start(f32[768,256]{1,0:T(8,128)S(1)} %get-tuple-element.16.w2_ref), channel_id=1, source_target_pairs={{0,127},{1,0},{2,1},{3,2},{4,3},{5,4},{6,5},{7,6},{8,7},{9,8},{10,... | collective-permute-start | bytes 2359304 | tf_op jit(solution)/shard_map/ppermute | solution.py:359
  117.8 44.8 %copy-start.7 = (s32[5]{0:T(128)}, s32[5]{0:T(128)S(1)}, u32[]{:S(2)}) copy-start(s32[5]{0:T(128)S(1)} %and_select_fusion.1.flag_ref) | copy-start | bytes 64
  119.1 43.6 %collective-permute-start.3 = (f32[768,256]{1,0:T(8,128)S(1)}, f32[768,256]{1,0:T(8,128)}, u32[]{:S(2)}, u32[]{:S(2)}) collective-permute-start(f32[768,256]{1,0:T(8,128)S(1)} %get-tuple-element.15.w1_ref), channel_id=1, source_target_pairs={{0,127},{1,0},{2,1},{3,2},{4,3},{5,4},{6,5},{7,6},{8,7},{9,8},{10,... | collective-permute-start | bytes 2359304 | tf_op jit(solution)/shard_map/ppermute | solution.py:359
  134.5 28.1 %copy-start.5 = (f32[768,256]{1,0:T(8,128)}, f32[768,256]{1,0:T(8,128)S(1)}, u32[]{:S(2)}) copy-start(f32[768,256]{1,0:T(8,128)S(1)} %collective-permute-done.1.m1w1_ref) | copy-start | bytes 2359300
  135.6 49.4 %collective-permute-start.6 = (f32[768,256]{1,0:T(8,128)}, f32[768,256]{1,0:T(8,128)}, u32[]{:S(2)}, u32[]{:S(2)}) collective-permute-start(f32[768,256]{1,0:T(8,128)} %broadcast_select_fusion), channel_id=1, source_target_pairs={{0,1},{1,2},{2,3},{3,4},{4,5},{5,6},{6,7},{7,8},{8,9},{9,10},{10,1... | collective-permute-start | bytes 2359304 | tf_op jit(solution)/shard_map/ppermute | solution.py:359
  151.5 33.5 %collective-permute-start.2 = (f32[768,256]{1,0:T(8,128)}, f32[768,256]{1,0:T(8,128)S(1)}, u32[]{:S(2)}, u32[]{:S(2)}) collective-permute-start(f32[768,256]{1,0:T(8,128)} %collective-permute-done.m1w0_ref), channel_id=1, source_target_pairs={{0,1},{1,2},{2,3},{3,4},{4,5},{5,6},{6,7},{7,8},{8,9},{9,10},{10,1... | collective-permute-start | bytes 2359304 | tf_op jit(solution)/shard_map/ppermute | solution.py:359
  151.5 33.5 %collective-permute-start.5 = (f32[768,256]{1,0:T(8,128)}, f32[768,256]{1,0:T(8,128)}, u32[]{:S(2)}, u32[]{:S(2)}) collective-permute-start(f32[768,256]{1,0:T(8,128)} %collective-permute-done.4.p1w2_ref), channel_id=1, source_target_pairs={{0,127},{1,0},{2,1},{3,2},{4,3},{5,4},{6,5},{7,6},{8,7},{9,8},{10,... | collective-permute-start | bytes 2359304 | tf_op jit(solution)/shard_map/ppermute | solution.py:359
  185.0 0.9 copy-start.6

commit v2 on v1

v2 whole, which is shorter than its diff:
```python
import jax
import jax.numpy as jnp
from jax import lax
from jax.experimental import pallas as pl
from jax.experimental.pallas import tpu as pltpu
from jax.sharding import PartitionSpec as P

F32 = jnp.float32
BF16 = jnp.bfloat16
AXES = ("gx", "gy")


def split2(x):
    hi = x.astype(BF16)
    lo = (x - hi.astype(F32)).astype(BF16)
    return hi, lo


def dg(x, y, dims=((1,), (0,))):
    return lax.dot_general(x, y, (dims, ((), ())), preferred_element_type=F32)


def dot3(x, y, dims=((1,), (0,))):
    return dg(x[0], y[0], dims) + (dg(x[0], y[1], dims) + dg(x[1], y[0], dims))


def pieces_of(strips_ref):
    pieces = []
    for i in range(3):
        x = strips_ref[i]
        hi = x.astype(BF16)
        rest = x - hi.astype(F32)
        mid = rest.astype(BF16)
        low = (rest - mid.astype(F32)).astype(BF16)
        pieces.append((hi, mid, low))
    return pieces


def hits_of(row, slot):
    n = row.shape[1]
    r_id = lax.broadcasted_iota(jnp.int32, (n, n), 0)
    c_id = lax.broadcasted_iota(jnp.int32, (n, n), 1)
    wide = jnp.broadcast_to(row, (n, n))
    same = jnp.where((wide.T == wide) & (r_id < c_id), 1, 0)
    within = jnp.sum(same, axis=0, keepdims=True)
    return [(within == slot) & (((row + shift) & (n - 1)) == r_id) for shift in range(4)]


def as_mask(cond):
    return jnp.where(cond, 1.0, 0.0).astype(BF16)


def pick(select, piece):
    hi, mid, low = piece
    return dg(select, hi) + (dg(select, mid) + dg(select, low))


def first_kernel(strips_ref, row_ref, out_ref):
    width = strips_ref.shape[2]
    pieces = pieces_of(strips_ref)
    for slot in range(2):
        hit = hits_of(row_ref[...], slot)
        for i in range(3):
            out_ref[:, slot, i * width : (i + 1) * width] = pick(as_mask(hit[i]), pieces[i])


def second_kernel(strips_ref, row_ref, flag_ref, out_ref):
    width = strips_ref.shape[2]
    n = row_ref.shape[1]
    pieces = pieces_of(strips_ref)
    flags = flag_ref[...]
    r_id = lax.broadcasted_iota(jnp.int32, (n, n), 0)
    c_id = lax.broadcasted_iota(jnp.int32, (n, n), 1)

    def flag_before(step):
        chosen = c_id == ((r_id + (n - step)) & (n - 1))
        return jnp.sum(jnp.where(chosen, flags, 0), axis=1, keepdims=True) > 0

    one_before = flag_before(1)
    two_before = flag_before(2)
    for slot in range(2):
        hit = hits_of(row_ref[...], slot)
        out_ref[:, slot, 0:width] = pick(as_mask(hit[1] & ~one_before), pieces[0]) + pick(
            as_mask(hit[3] & one_before), pieces[1]
        )
        out_ref[:, slot, width : 2 * width] = pick(as_mask(hit[2]), pieces[1])
        out_ref[:, slot, 2 * width : 3 * width] = pick(
            as_mask(hit[2] & ~two_before), pieces[0]
        ) + pick(as_mask(hit[3] & two_before), pieces[2])


def bucket(kernel, name, *args):
    n, wide = args[0].shape[1], 3 * args[0].shape[2]
    return pl.pallas_call(
        kernel,
        out_shape=jax.ShapeDtypeStruct((n, 2, wide), F32),
        cost_estimate=pl.CostEstimate(
            flops=10 * n * n * wide, bytes_accessed=12 * n * wide, transcendentals=0
        ),
        name=name,
    )(*args)


def chol_block(a):
    n = a.shape[0]
    groups = n // 8
    sub = lax.broadcasted_iota(jnp.int32, (8, n), 0)
    lane = lax.broadcasted_iota(jnp.int32, (8, n), 1)
    left = [a[8 * v : 8 * v + 8, :] for v in range(groups)]
    right = [jnp.where(lane == sub + 8 * v, 1.0, 0.0).astype(F32) for v in range(groups)]

    def lanes_of(x, k):
        return [jnp.broadcast_to(x[:, 8 * k + i : 8 * k + i + 1], (8, n)) for i in range(8)]

    def sub_of(x, i):
        return jnp.broadcast_to(x[i : i + 1, :], (8, n))

    for k in range(groups):
        c = lanes_of(left[k], k)
        u, v_in = left[k], right[k]
        scale, row_u, row_v, row_c = [], [], [], []
        for i in range(8):
            inv = lax.rsqrt(sub_of(c[i], i))
            ru = sub_of(u, i) * inv
            rv = sub_of(v_in, i) * inv
            rc = [None] * 8
            m = jnp.where(sub > i, c[i] * inv, 0.0)
            for j in range(i + 1, 8):
                rc[j] = sub_of(c[j], i) * inv
                c[j] = c[j] - m * rc[j]
            u = jnp.where(sub == i, ru, u - m * ru)
            v_in = jnp.where(sub == i, rv, v_in - m * rv)
            scale.append(inv)
            row_u.append(ru)
            row_v.append(rv)
            row_c.append(rc)
        left[k], right[k] = u, v_in
        for g in range(k + 1, groups):
            c = lanes_of(left[g], k)
            x, y = left[g], right[g]
            for i in range(8):
                m = c[i] * scale[i]
                for j in range(i + 1, 8):
                    c[j] = c[j] - m * row_c[i][j]
                x = x - m * row_u[i]
                y = y - m * row_v[i]
            left[g], right[g] = x, y
    upper = jnp.concatenate(left, axis=0)
    r_id = lax.broadcasted_iota(jnp.int32, (n, n), 0)
    c_id = lax.broadcasted_iota(jnp.int32, (n, n), 1)
    return jnp.where(c_id >= r_id, upper, 0.0), jnp.concatenate(right, axis=0)


MESH = pl.DeviceIdType.MESH


def chol_kernel(
    recv_ref, shift_ref, flag_ref,
    l_ref, w1_ref, w2_ref, ath_ref, atl_ref, c_ref, f_ref,
    m1w0_ref, m1w1_ref, m2w0_ref, p1w1_ref, p1w2_ref, p2w2_ref, gx_ref, gy_ref,
    m_ref, x_ref, w0_ref, ah_ref, al_ref, outx_ref, outy_ref, gram_ref,
    send_sem, recv_sem, small_send, small_recv,
):
    size = shift_ref.shape[1]
    slots = w0_ref.shape[1]
    half = slots // 2
    nb = 128
    count = size // nb
    rows_y = lax.axis_size("gy")
    total_dev = lax.axis_size("gx") * rows_y
    own = lax.axis_index("gx") * rows_y + lax.axis_index("gy")
    up = lax.rem(own + 1, total_dev)
    down = lax.rem(own + total_dev - 1, total_dev)
    up_id = (lax.div(up, rows_y), lax.rem(up, rows_y))
    down_id = (lax.div(down, rows_y), lax.rem(down, rows_y))

    barrier = pltpu.get_barrier_semaphore()
    for there in (up_id, down_id):
        pl.semaphore_signal(barrier, inc=1, device_id=there, device_id_type=MESH)

    def rows(k):
        return pl.ds(pl.multiple_of(k * nb, nb), nb)

    def copy(which, k):
        source, target, there = (
            (w0_ref, m1w0_ref, up_id),
            (w1_ref, m1w1_ref, up_id),
            (m1w0_ref, m2w0_ref, up_id),
            (w1_ref, p1w1_ref, down_id),
            (w2_ref, p1w2_ref, down_id),
            (p1w2_ref, p2w2_ref, down_id),
        )[which]
        return pltpu.make_async_remote_copy(
            src_ref=source.at[rows(k), :],
            dst_ref=target.at[rows(k), :],
            send_sem=send_sem.at[which, k],
            recv_sem=recv_sem.at[which, k],
            device_id=there,
            device_id_type=MESH,
        )

    def small(which):
        source, target = ((outx_ref, gx_ref), (outy_ref, gy_ref))[which]
        return pltpu.make_async_remote_copy(
            src_ref=source,
            dst_ref=target,
            send_sem=small_send.at[which],
            recv_sem=small_recv.at[which],
            device_id=up_id,
            device_id_type=MESH,
        )

    def relay(k):
        copy(0, k).wait_recv()
        copy(2, k).start()
        copy(4, k).wait_recv()
        copy(5, k).start()

    l_ref[...] = jnp.zeros_like(l_ref)
    f_ref[...] = jnp.zeros_like(f_ref)
    gram_ref[...] = jnp.zeros_like(gram_ref)
    for i in range(3):
        for s in range(2):
            x = recv_ref[:, s, i * size : (i + 1) * size]
            hi, lo = split2(x)
            ah_ref[i, s * half : (s + 1) * half, :] = hi
            al_ref[i, s * half : (s + 1) * half, :] = lo
            at = x.T
            begin = i * slots + s * half
            m_ref[:, size + begin : size + begin + half] = at
            hi, lo = split2(at)
            ath_ref[:, begin : begin + half] = hi
            atl_ref[:, begin : begin + half] = lo
    for blk in range(0, size, 256):
        total = None
        for i in range(3):
            a = (ah_ref[i, :, blk : blk + 256], al_ref[i, :, blk : blk + 256])
            t = (ath_ref[:, i * slots : (i + 1) * slots], atl_ref[:, i * slots : (i + 1) * slots])
            add = dot3(t, a)
            total = add if total is None else total + add
        r_id = lax.broadcasted_iota(jnp.int32, (size, 256), 0)
        c_id = lax.broadcasted_iota(jnp.int32, (size, 256), 1) + blk
        m_ref[:, blk : blk + 256] = total + jnp.where(
            r_id == c_id, shift_ref[:, blk : blk + 256], 0.0
        )
    pl.semaphore_wait(barrier, 2)

    w_refs = (w0_ref, w1_ref, w2_ref)

    def step(k, carry):
        at = pl.multiple_of(k * nb, nb)
        upper, inverse = chol_block(m_ref[pl.ds(at, nb), pl.ds(at, nb)])
        l_ref[pl.ds(at, nb), pl.ds(at, nb)] = upper.T
        inv = split2(inverse)
        for blk in range(0, 2 * size, 256):
            x_ref[:, blk : blk + 256] = dot3(inv, split2(m_ref[pl.ds(at, nb), blk : blk + 256]))
        for i in range(3):
            w_refs[i][pl.ds(at, nb), :] = x_ref[:, size + i * slots : size + (i + 1) * slots]

        def trail(r, inner):
            to = pl.multiple_of(r * nb, nb)
            low = x_ref[:, pl.ds(to, nb)].T
            l_ref[pl.ds(to, nb), pl.ds(at, nb)] = low
            low = split2(low)
            for blk in range(0, 2 * size, 256):
                m_ref[pl.ds(to, nb), blk : blk + 256] -= dot3(
                    low, split2(x_ref[:, blk : blk + 256])
                )
            return inner

        lax.fori_loop(k + 1, count, trail, carry)
        wt = split2(x_ref[:, size + 2 * slots : size + 3 * slots].T)
        for j in range(2):
            gram_ref[j] += dot3(wt, split2(x_ref[:, size + j * slots : size + (j + 1) * slots]))
        for which in (0, 4, 1, 3):
            copy(which, k).start()

        @pl.when(k >= 2)
        def _():
            relay(k - 2)

        return carry

    lax.fori_loop(0, count, step, 0)

    flag = [flag_ref[i : i + 1, 0:1] for i in range(5)]
    outx_ref[...] = gram_ref[0] * flag[2]

    def a_of(i):
        return ah_ref[i], al_ref[i]

    def near(k, carry):
        copy(1, k).wait_recv()
        copy(3, k).wait_recv()

        @pl.when(k >= count - 2)
        def _():
            relay(k)

        p1w1, p1w2 = p1w1_ref[rows(k), :], p1w2_ref[rows(k), :]
        m1w0, m1w1 = m1w0_ref[rows(k), :], m1w1_ref[rows(k), :]
        c = dot3(split2(p1w1), a_of(0)) + dot3(split2(p1w2), a_of(1))
        c_ref[1, rows(k), :] = c
        c = split2(c * flag[3])
        f_ref[0] += dot3(split2(p1w1.T), c)
        f_ref[1] += dot3(split2(p1w2.T), c)
        m1w0s = split2(m1w0)
        c = dot3(m1w0s, a_of(1)) + dot3(split2(m1w1), a_of(2))
        c_ref[2, rows(k), :] = c
        c = split2(c * flag[1])
        w1t = split2(m1w1.T)
        f_ref[1] += dot3(split2(m1w0.T), c)
        f_ref[2] += dot3(w1t, c)
        gram_ref[2] += dot3(w1t, m1w0s)

        @pl.when(k == 0)
        def _():
            small(0).start()

        return carry

    lax.fori_loop(0, count, near, 0)
    outy_ref[...] = gram_ref[1] * flag[2] + gram_ref[2] * (1.0 - flag[2])

    def far(k, carry):
        copy(2, k).wait_recv()
        copy(5, k).wait_recv()
        w = p2w2_ref[rows(k), :]
        c = dot3(split2(w), a_of(0))
        c_ref[0, rows(k), :] = c
        f_ref[0] += dot3(split2(w.T), split2(c * flag[4]))
        w = m2w0_ref[rows(k), :]
        c = dot3(split2(w), a_of(2))
        c_ref[3, rows(k), :] = c
        f_ref[2] += dot3(split2(w.T), split2(c * flag[0]))

        @pl.when(k == 0)
        def _():
            small(1).start()

        return carry

    lax.fori_loop(0, count, far, 0)
    for which in range(2):
        small(which).wait_recv()
    f_ref[3] = dot3(split2(gx_ref[...]), a_of(1)) + dot3(split2(gy_ref[...]), a_of(2))
    for which in range(2):
        small(which).wait_send()

    def drain(k, carry):
        for which in range(6):
            copy(which, k).wait_send()
        return carry

    lax.fori_loop(0, count, drain, 0)


def chol(recv, shift, flags):
    size = shift.shape[1]
    slots = 2 * recv.shape[0]
    w = jax.ShapeDtypeStruct((size, slots), F32)
    low = jax.ShapeDtypeStruct((size, 3 * slots), BF16)
    square = jax.ShapeDtypeStruct((slots, slots), F32)
    count = size // 128
    return pl.pallas_call(
        chol_kernel,
        out_shape=(
            jax.ShapeDtypeStruct((size, size), F32), w, w, low, low,
            jax.ShapeDtypeStruct((4, size, size), F32),
            jax.ShapeDtypeStruct((4, slots, size), F32),
        ),
        scratch_shapes=[pltpu.VMEM((size, slots), F32)] * 6
        + [pltpu.VMEM((slots, slots), F32)] * 2
        + [
            pltpu.VMEM((size, size + 3 * slots), F32),
            pltpu.VMEM((128, size + 3 * slots), F32),
            pltpu.VMEM((size, slots), F32),
            pltpu.VMEM((3, slots, size), BF16),
            pltpu.VMEM((3, slots, size), BF16),
            pltpu.VMEM((slots, slots), F32),
            pltpu.VMEM((slots, slots), F32),
            pltpu.VMEM((3, slots, slots), F32),
            pltpu.SemaphoreType.DMA((6, count)),
            pltpu.SemaphoreType.DMA((6, count)),
            pltpu.SemaphoreType.DMA((2,)),
            pltpu.SemaphoreType.DMA((2,)),
        ],
        compiler_params=pltpu.CompilerParams(
            vmem_limit_bytes=56 * 2**20, collective_id=0, has_side_effects=True
        ),
        cost_estimate=pl.CostEstimate(
            flops=30 * size * size * size, bytes_accessed=30 * size * size, transcendentals=0
        ),
        name="chol",
    )(recv, shift, flags)


def last_kernel(
    flag_ref, recv_ref, ath_ref, atl_ref, q_ref, shift_ref, l_ref, w1_ref, w2_ref, c_ref, f_ref,
    schur_ref, coup_ref, qh_ref, ql_ref, sem,
):
    step = pl.program_id(0)
    size = shift_ref.shape[1]
    slots = w1_ref.shape[1]
    half = slots // 2
    cols = schur_ref.shape[3]
    fm2, fm1, own = [flag_ref[i] > 0 for i in range(3)]
    out = pltpu.make_async_copy(c_ref, coup_ref.at[0], sem)

    @pl.when(step == 0)
    def _():
        out.start()
        for i in range(3):
            for s in range(2):
                begin = i * slots + s * half
                hi, lo = split2(q_ref[:, s, i * size : (i + 1) * size].T)
                qh_ref[:, begin : begin + half] = hi
                ql_ref[:, begin : begin + half] = lo

    base = pl.multiple_of(step * cols, cols)
    span = pl.ds(base, cols)

    def at_of(i):
        return ath_ref[:, i * slots : (i + 1) * slots], atl_ref[:, i * slots : (i + 1) * slots]

    def q_of(i):
        return qh_ref[:, i * slots : (i + 1) * slots], ql_ref[:, i * slots : (i + 1) * slots]

    @pl.when(own)
    def _():
        w1 = split2(w1_ref[span, :])
        w2 = split2(w2_ref[span, :])
        over = ((1,), (1,))
        schur_ref[0, 0] = dot3(q_of(2), w2, over)
        schur_ref[0, 1] = dot3(q_of(0), w1, over) + dot3(q_of(1), w2, over)
        schur_ref[0, 2] = l_ref[:, span]

    @pl.when(jnp.logical_not(own))
    def _():
        y = []
        for i in range(3):
            lanes = pl.ds(pl.multiple_of(i * size + base, cols), cols)
            a = jnp.concatenate([recv_ref[:, 0, lanes], recv_ref[:, 1, lanes]], axis=0)
            y.append(split2(a - f_ref[i, :, span]))
        r_id = lax.broadcasted_iota(jnp.int32, (size, cols), 0)
        c_id = lax.broadcasted_iota(jnp.int32, (size, cols), 1) + base
        diag = jnp.where(r_id == c_id, shift_ref[:, span], 0.0)
        schur_ref[0, 2] = (
            dot3(at_of(0), y[0]) + dot3(at_of(1), y[1]) + dot3(at_of(2), y[2])
        ) + diag

        @pl.when(fm1)
        def _():
            schur_ref[0, 1] = c_ref[2, :, span]

        @pl.when(jnp.logical_not(fm1))
        def _():
            schur_ref[0, 1] = dot3(q_of(0), y[1]) + dot3(q_of(1), y[2])

            @pl.when(fm2)
            def _():
                schur_ref[0, 1] -= dot3(q_of(2), split2(f_ref[3, :, span]))

        @pl.when(fm2)
        def _():
            schur_ref[0, 0] = c_ref[3, :, span]

        @pl.when(jnp.logical_not(fm2))
        def _():
            schur_ref[0, 0] = dot3(q_of(2), y[2])

            @pl.when(fm1)
            def _():
                schur_ref[0, 0] -= dot3(q_of(0), split2(f_ref[3, :, span]))

    @pl.when(step == pl.num_programs(0) - 1)
    def _():
        out.wait()


def last(flags, recv, q, shift, l, w1, w2, ath, atl, c, f):
    size = shift.shape[1]
    slots = w1.shape[1]
    cols = 256
    whole = pl.BlockSpec(memory_space=pltpu.VMEM)
    return pl.pallas_call(
        last_kernel,
        grid=(size // cols,),
        in_specs=[pl.BlockSpec(memory_space=pltpu.SMEM)] + [whole] * 10,
        out_specs=(
            pl.BlockSpec((1, 3, size, cols), lambda n: (0, 0, 0, n)),
            pl.BlockSpec(memory_space=pl.ANY),
        ),
        out_shape=(
            jax.ShapeDtypeStruct((1, 3, size, size), F32),
            jax.ShapeDtypeStruct((1, 4, size, size), F32),
        ),
        scratch_shapes=[
            pltpu.VMEM((size, 3 * slots), BF16),
            pltpu.VMEM((size, 3 * slots), BF16),
            pltpu.SemaphoreType.DMA,
        ],
        compiler_params=pltpu.CompilerParams(vmem_limit_bytes=44 * 2**20),
        name="last",
    )(flags, recv, ath, atl, q, shift, l, w1, w2, c, f)


def exchange(payload):
    return lax.all_to_all(payload, AXES, split_axis=0, concat_axis=0, tiled=True)


def local(strips, index, shift, flags):
    count = lax.axis_size(AXES)
    own = lax.axis_index(AXES)
    strips = jnp.transpose(strips, (1, 0, 2))
    index = index.reshape(1, -1)
    first = bucket(first_kernel, "first", strips, index)
    recv = exchange(first)
    second = bucket(second_kernel, "second", strips, index, flags.reshape(1, -1))
    near = jnp.take(flags, (own + jnp.arange(-2, 6)) % count)
    wide = jnp.broadcast_to(near.astype(F32)[:, None], (8, 128))
    parts = chol(recv, shift, wide)
    q = exchange(second)
    return last(near, recv, q, shift, *parts)


def solution(mesh):
    in_specs = (P(AXES, None, None), P(AXES, None), P(AXES, None), P())
    out_specs = (P(AXES, None, None, None), P(AXES, None, None, None))
    return jax.shard_map(local, mesh=mesh, in_specs=in_specs, out_specs=out_specs, check_vma=False)
```

time: 215 us -> 177 us (0.82)
  waiting for transfers between devices: 81.3 us -> 27.7 us
  Pallas kernels: 76.2 us -> 125 us
  starting transfers between devices: 33 us -> 17.1 us
  local copies, waits for them, and re-layouts: 21.7 us -> 6.12 us
    pallas_call x1, Pallas kernels: 41.9 us -> 100 us  [chol(): pl.pallas_call(chol_kernel, out_shape=(jax.ShapeDtypeStruct((size, size),...]
    ppermute x7 -> x0, waiting for transfers between devices: 52.7 us -> none  [passed_along(): return lax.ppermute(value, AXES, pairs)]
    ppermute x7 -> x0, starting transfers between devices: 15.9 us -> none  [passed_along(): return lax.ppermute(value, AXES, pairs)]
    reshape x5 -> x0, local copies, waits for them, and re-layouts: 15.5 us -> none  [the longest x2 7.53 us: exchange(): payload.reshape(count, -1, wide)]
    pallas_call x1, Pallas kernels: 28.9 us -> 16.3 us  [last(): pl.pallas_call(last_kernel, grid=(size // cols,), in_specs=[pl.BlockSpec(...]
    pallas_call x1 -> x2, Pallas kernels: 5.45 us -> 8.71 us  [bucket(): pl.pallas_call(kernel, out_shape=jax.ShapeDtypeStruct((n, 2, wide), F32),...]
    unnamed x18 -> x16, local copies, waits for them, and re-layouts: 4.96 us -> 4.81 us
  transfers between devices with their start and end apart: 9 -> 2, of which waited for: 4 -> 1; matrix products, arithmetic and copies ran while one was open for 6% -> 1% of each run, Pallas kernels for 19% -> 59%
where the time goes in v2:
time: 177 us
  Pallas kernels  125 us (71%)
  waiting for transfers between devices  27.7 us (16%)
  starting transfers between devices  17.1 us (10%)
  local copies, waits for them, and re-layouts  6.12 us (3%)
    pallas_call x1, Pallas kernels, chol(): pl.pallas_call(chol_kernel, out_shape=(jax.ShapeDtypeStruct((size, size),...  100 us
    all_to_all x2, waiting for transfers between devices, exchange(): lax.all_to_all(payload, AXES, split_axis=0, concat_axis=0, tiled=True)  27.7 us
    all_to_all x2, starting transfers between devices, exchange(): lax.all_to_all(payload, AXES, split_axis=0, concat_axis=0, tiled=True)  17.1 us
    pallas_call x1, Pallas kernels, last(): pl.pallas_call(last_kernel, grid=(size // cols,), in_specs=[pl.BlockSpec(...  16.3 us
    pallas_call x2, Pallas kernels, bucket(): pl.pallas_call(kernel, out_shape=jax.ShapeDtypeStruct((n, 2, wide), F32),...  8.71 us
    unnamed x16, local copies, waits for them, and re-layouts  4.81 us
  transfers between devices with their start and end apart: 2, of which 1 were waited for; matrix products, arithmetic and copies ran while one was open for 1% of the time, Pallas kernels for 59%

profile of v2, /device:TPU:0, one launch (start us, length us, event | category | flops | bytes accessed | tf_op | source)
XLA Modules:
  0.0 176.9 jit_solution(366804047366888085)
XLA Ops:
  0.6 4.0 %first.1 = f32[128,2,2304]{2,1,0:T(2,128)} custom-call(f32[3,128,768]{2,1,0:T(8,128)} %bitcast.6, s32[1,128]{1,0:T(1,128)} %bitcast.8), custom_call_target="tpu_custom_call" | custom-call | flops 377487360 | bytes 3538944 | tf_op jit(solution)/shard_map/first/pallas_call | solution.py:94
  4.7 11.2 %all-to-all-start = ((f32[128,2,2304]{2,1,0:T(2,128)}), f32[128,2,2304]{2,1,0:T(2,128)S(1)}, u32[]{:S(2)}, u32[]{:S(2)}) async-start(f32[128,2,2304]{2,1,0:T(2,128)} %first.1), calls=%async_computation | async-start | bytes 4718592 | tf_op jit(solution)/shard_map/all_to_all | solution.py:509
  15.8 4.7 %second.1 = f32[128,2,2304]{2,1,0:T(2,128)} custom-call(f32[3,128,768]{2,1,0:T(8,128)} %bitcast.7, s32[1,128]{1,0:T(1,128)} %bitcast.9, s32[1,128]{1,0:T(1,128)} %bitcast.5), custom_call_target="tpu_custom_call" | custom-call | flops 377487360 | bytes 3538944 | tf_op jit(solution)/shard_map/second/pallas_call | solution.py:94
  20.5 0.0 copy-start.7
  20.5 27.7 %all-to-all-done.recv_ref = f32[128,2,2304]{2,1,0:T(2,128)S(1)} async-done(((f32[128,2,2304]{2,1,0:T(2,128)}), f32[128,2,2304]{2,1,0:T(2,128)S(1)}, u32[]{:S(2)}, u32[]{:S(2)}) %all-to-all-start) | async-done | bytes 2359328 | tf_op jit(solution)/shard_map/all_to_all | solution.py:509
  48.3 0.0 copy-start
  48.3 5.9 %all-to-all-start.1 = ((f32[128,2,2304]{2,1,0:T(2,128)}), f32[128,2,2304]{2,1,0:T(2,128)}, u32[]{:S(2)}, u32[]{:S(2)}) async-start(f32[128,2,2304]{2,1,0:T(2,128)} %second.1), calls=%async_computation.1 | async-start | bytes 4718592 | tf_op jit(solution)/shard_map/all_to_all | solution.py:509
  54.2 0.0 copy-done
  54.3 0.0 copy-done.7
  54.3 0.6 gather_fusion
  54.9 0.7 broadcast_in_dim.4.flag_ref
  55.6 0.0 copy-start.1
  55.6 0.0 copy-start.6
  55.6 100.0 %chol.1 = (f32[768,768]{1,0:T(8,128)}, f32[768,256]{1,0:T(8,128)}, f32[768,256]{1,0:T(8,128)}, bf16[768,768]{1,0:T(8,128)(2,1)}, bf16[768,768]{1,0:T(8,128)(2,1)...) custom-call(f32[128,2,2304]{2,1,0:T(2,128)} %copy-done, f32[1,768]{1,0:T(1,128)} %shift_ref.3, ...), custom_call_target="tpu_custom_call" | custom-call | flops 13589544960 | bytes 17694720 | tf_op jit(solution)/shard_map/chol/pallas_call | solution.py:365
  155.6 0.0 all-to-all-done.1.q_ref
  155.6 0.0 copy-done.1
  155.6 0.0 copy-done.6
  155.6 0.0 copy-start.2
  155.6 1.3 copy-done.2
  156.9 0.0 copy-start.3
  156.9 1.3 copy-done.3
  158.1 0.0 copy-start.4
  158.1 1.1 copy-done.4
  159.3 0.0 copy-start.5
  159.3 1.1 copy-done.5
  160.4 16.3 %last.1 = (f32[1,3,768,768]{3,2,1,0:T(8,128)}, f32[1,4,768,768]{3,2,1,0:T(8,128)}) custom-call(s32[8]{0:T(128)S(1)} %get-tuple-element.17.flag_ref, f32[128,2,2304]{2,1,0:T(2,128)S(1)} %copy-done.1, bf16[768,768]{1,0:T(8,128)(2,1)S(1)} %copy-done.2, bf16[768,768]{1,0:T(8,128)(2,1)S(1)} %copy-done.3, f32[128,2,2304]{2,1,0:T(2,128)} %all-to-all-done.1.q_ref, ...), custom_call_target="tpu_custom_call" | custom-call | tf_op jit(solution)/shard_map/last/pallas_call | solution.py:486
  (3 shorter events, 0.0 us)
Async XLA Ops:
  4.7 43.6 %all-to-all-start = ((f32[128,2,2304]{2,1,0:T(2,128)}), f32[128,2,2304]{2,1,0:T(2,128)S(1)}, u32[]{:S(2)}, u32[]{:S(2)}) async-start(f32[128,2,2304]{2,1,0:T(2,128)} %first.1), calls=%async_computation | async-start | bytes 4718592 | tf_op jit(solution)/shard_map/all_to_all | solution.py:509
  20.5 33.7 %copy-start.7 = (s32[128]{0:T(128)S(1)}, s32[128]{0:T(128)}, u32[]{:S(2)}) copy-start(s32[128]{0:T(128)} %param.7) | copy-start | bytes 1540
  48.3 6.0 %copy-start = (f32[128,2,2304]{2,1,0:T(2,128)}, f32[128,2,2304]{2,1,0:T(2,128)S(1)}, u32[]{:S(2)}) copy-start(f32[128,2,2304]{2,1,0:T(2,128)S(1)} %all-to-all-done.recv_ref) | copy-start | bytes 7077892
  48.3 107.3 %all-to-all-start.1 = ((f32[128,2,2304]{2,1,0:T(2,128)}), f32[128,2,2304]{2,1,0:T(2,128)}, u32[]{:S(2)}, u32[]{:S(2)}) async-start(f32[128,2,2304]{2,1,0:T(2,128)} %second.1), calls=%async_computation.1 | async-start | bytes 4718592 | tf_op jit(solution)/shard_map/all_to_all | solution.py:509
  55.6 100.0 %copy-start.1 = (f32[128,2,2304]{2,1,0:T(2,128)S(1)}, f32[128,2,2304]{2,1,0:T(2,128)}, u32[]{:S(2)}) copy-start(f32[128,2,2304]{2,1,0:T(2,128)} %copy-done) | copy-start | bytes 7077892
  55.6 100.0 %copy-start.6 = (f32[1,768]{1,0:T(1,128)S(1)}, f32[1,768]{1,0:T(1,128)}, u32[]{:S(2)}) copy-start(f32[1,768]{1,0:T(1,128)} %shift_ref.3) | copy-start | bytes 9220
  155.6 1.3 copy-start.2
  156.9 1.3 copy-start.3
  158.1 1.1 copy-start.4
  159.3 1.1 copy-start.5

commit v3 on v2

--- a/solution.py
+++ b/solution.py
@@ -22,6 +22,11 @@
 
 def dot3(x, y, dims=((1,), (0,))):
     return dg(x[0], y[0], dims) + (dg(x[0], y[1], dims) + dg(x[1], y[0], dims))
+
+
+def dot3_short(x, y):
+    both = dg(jnp.concatenate(x, axis=1), jnp.concatenate([y[0], y[0]], axis=0))
+    return both + dg(x[0], y[1])
 
 
 def pieces_of(strips_ref):
@@ -156,10 +161,11 @@
 
 def chol_kernel(
     recv_ref, shift_ref, flag_ref,
-    l_ref, w1_ref, w2_ref, ath_ref, atl_ref, c_ref, f_ref,
+    l_ref, w1_ref, w2_ref, ath_ref, atl_ref, cout_ref, f_ref,
+    c_ref,
     m1w0_ref, m1w1_ref, m2w0_ref, p1w1_ref, p1w2_ref, p2w2_ref, gx_ref, gy_ref,
     m_ref, x_ref, w0_ref, ah_ref, al_ref, outx_ref, outy_ref, gram_ref,
-    send_sem, recv_sem, small_send, small_recv,
+    send_sem, recv_sem, small_send, small_recv, c_sem,
 ):
     size = shift_ref.shape[1]
     slots = w0_ref.shape[1]
@@ -235,12 +241,13 @@
         total = None
         for i in range(3):
             a = (ah_ref[i, :, blk : blk + 256], al_ref[i, :, blk : blk + 256])
-            t = (ath_ref[:, i * slots : (i + 1) * slots], atl_ref[:, i * slots : (i + 1) * slots])
+            here = slice(i * slots, (i + 1) * slots)
+            t = (ath_ref[0 : blk + 256, here], atl_ref[0 : blk + 256, here])
             add = dot3(t, a)
             total = add if total is None else total + add
-        r_id = lax.broadcasted_iota(jnp.int32, (size, 256), 0)
-        c_id = lax.broadcasted_iota(jnp.int32, (size, 256), 1) + blk
-        m_ref[:, blk : blk + 256] = total + jnp.where(
+        r_id = lax.broadcasted_iota(jnp.int32, (blk + 256, 256), 0)
+        c_id = lax.broadcasted_iota(jnp.int32, (blk + 256, 256), 1) + blk
+        m_ref[0 : blk + 256, blk : blk + 256] = total + jnp.where(
             r_id == c_id, shift_ref[:, blk : blk + 256], 0.0
         )
     pl.semaphore_wait(barrier, 2)
@@ -252,8 +259,17 @@
         upper, inverse = chol_block(m_ref[pl.ds(at, nb), pl.ds(at, nb)])
         l_ref[pl.ds(at, nb), pl.ds(at, nb)] = upper.T
         inv = split2(inverse)
-        for blk in range(0, 2 * size, 256):
-            x_ref[:, blk : blk + 256] = dot3(inv, split2(m_ref[pl.ds(at, nb), blk : blk + 256]))
+        for blk in range(size, 2 * size, 256):
+            x_ref[:, blk : blk + 256] = dot3_short(
+                inv, split2(m_ref[pl.ds(at, nb), blk : blk + 256])
+            )
+        for blk in range(0, size, 256):
+
+            @pl.when(blk + 256 > at + nb)
+            def _(blk=blk):
+                x_ref[:, blk : blk + 256] = dot3_short(
+                    inv, split2(m_ref[pl.ds(at, nb), blk : blk + 256])
+                )
         for i in range(3):
             w_refs[i][pl.ds(at, nb), :] = x_ref[:, size + i * slots : size + (i + 1) * slots]
 
@@ -262,16 +278,26 @@
             low = x_ref[:, pl.ds(to, nb)].T
             l_ref[pl.ds(to, nb), pl.ds(at, nb)] = low
             low = split2(low)
-            for blk in range(0, 2 * size, 256):
-                m_ref[pl.ds(to, nb), blk : blk + 256] -= dot3(
+            for blk in range(size, 2 * size, 256):
+                m_ref[pl.ds(to, nb), blk : blk + 256] -= dot3_short(
                     low, split2(x_ref[:, blk : blk + 256])
                 )
+            for blk in range(0, size, 256):
+
+                @pl.when(blk + 256 > to)
+                def _(blk=blk):
+                    m_ref[pl.ds(to, nb), blk : blk + 256] -= dot3_short(
+                        low, split2(x_ref[:, blk : blk + 256])
+                    )
+
             return inner
 
         lax.fori_loop(k + 1, count, trail, carry)
         wt = split2(x_ref[:, size + 2 * slots : size + 3 * slots].T)
         for j in range(2):
-            gram_ref[j] += dot3(wt, split2(x_ref[:, size + j * slots : size + (j + 1) * slots]))
+            gram_ref[j] += dot3_short(
+                wt, split2(x_ref[:, size + j * slots : size + (j + 1) * slots])
+            )
         for which in (0, 4, 1, 3):
             copy(which, k).start()
 
@@ -289,63 +315,80 @@
     def a_of(i):
         return ah_ref[i], al_ref[i]
 
+    def out_copy(which, k):
+        return pltpu.make_async_copy(
+            c_ref.at[which, wide(k), :], cout_ref.at[which, wide(k), :], c_sem.at[which, k]
+        )
+
+    def wide(k):
+        return pl.ds(pl.multiple_of(k * 2 * nb, 2 * nb), 2 * nb)
+
     def near(k, carry):
-        copy(1, k).wait_recv()
-        copy(3, k).wait_recv()
-
-        @pl.when(k >= count - 2)
-        def _():
-            relay(k)
-
-        p1w1, p1w2 = p1w1_ref[rows(k), :], p1w2_ref[rows(k), :]
-        m1w0, m1w1 = m1w0_ref[rows(k), :], m1w1_ref[rows(k), :]
+        for part in range(2):
+            copy(1, 2 * k + part).wait_recv()
+            copy(3, 2 * k + part).wait_recv()
+
+        @pl.when(k >= 1)
+        def _():
+            relay(k + 3)
+
+        p1w1, p1w2 = p1w1_ref[wide(k), :], p1w2_ref[wide(k), :]
         c = dot3(split2(p1w1), a_of(0)) + dot3(split2(p1w2), a_of(1))
-        c_ref[1, rows(k), :] = c
+        c_ref[1, wide(k), :] = c
         c = split2(c * flag[3])
         f_ref[0] += dot3(split2(p1w1.T), c)
         f_ref[1] += dot3(split2(p1w2.T), c)
+
+        @pl.when(k == 0)
+        def _():
+            small(0).start()
+
+        m1w0, m1w1 = m1w0_ref[wide(k), :], m1w1_ref[wide(k), :]
         m1w0s = split2(m1w0)
         c = dot3(m1w0s, a_of(1)) + dot3(split2(m1w1), a_of(2))
-        c_ref[2, rows(k), :] = c
+        c_ref[2, wide(k), :] = c
         c = split2(c * flag[1])
         w1t = split2(m1w1.T)
         f_ref[1] += dot3(split2(m1w0.T), c)
         f_ref[2] += dot3(w1t, c)
         gram_ref[2] += dot3(w1t, m1w0s)
+        out_copy(1, k).start()
+        out_copy(2, k).start()
+        return carry
+
+    lax.fori_loop(0, count // 2, near, 0)
+    outy_ref[...] = gram_ref[1] * flag[2] + gram_ref[2] * (1.0 - flag[2])
+
+    def far(k, carry):
+        for part in range(2):
+            copy(2, 2 * k + part).wait_recv()
+            copy(5, 2 * k + part).wait_recv()
+        w = p2w2_ref[wide(k), :]
+        c = dot3(split2(w), a_of(0))
+        c_ref[0, wide(k), :] = c
+        f_ref[0] += dot3(split2(w.T), split2(c * flag[4]))
 
         @pl.when(k == 0)
         def _():
-            small(0).start()
-
+            small(1).start()
+
+        w = m2w0_ref[wide(k), :]
+        c = dot3(split2(w), a_of(2))
+        c_ref[3, wide(k), :] = c
+        f_ref[2] += dot3(split2(w.T), split2(c * flag[0]))
+        out_copy(0, k).start()
+        out_copy(3, k).start()
         return carry
 
-    lax.fori_loop(0, count, near, 0)
-    outy_ref[...] = gram_ref[1] * flag[2] + gram_ref[2] * (1.0 - flag[2])
-
-    def far(k, carry):
-        copy(2, k).wait_recv()
-        copy(5, k).wait_recv()
-        w = p2w2_ref[rows(k), :]
-        c = dot3(split2(w), a_of(0))
-        c_ref[0, rows(k), :] = c
-        f_ref[0] += dot3(split2(w.T), split2(c * flag[4]))
-        w = m2w0_ref[rows(k), :]
-        c = dot3(split2(w), a_of(2))
-        c_ref[3, rows(k), :] = c
-        f_ref[2] += dot3(split2(w.T), split2(c * flag[0]))
-
-        @pl.when(k == 0)
-        def _():
-            small(1).start()
-
-        return carry
-
-    lax.fori_loop(0, count, far, 0)
+    lax.fori_loop(0, count // 2, far, 0)
     for which in range(2):
         small(which).wait_recv()
     f_ref[3] = dot3(split2(gx_ref[...]), a_of(1)) + dot3(split2(gy_ref[...]), a_of(2))
     for which in range(2):
         small(which).wait_send()
+    for which in range(4):
+        for k in range(count // 2):
+            out_copy(which, k).wait()
 
     def drain(k, carry):
         for which in range(6):
@@ -362,6 +405,7 @@
     low = jax.ShapeDtypeStruct((size, 3 * slots), BF16)
     square = jax.ShapeDtypeStruct((slots, slots), F32)
     count = size // 128
+    whole = pl.BlockSpec(memory_space=pltpu.VMEM)
     return pl.pallas_call(
         chol_kernel,
         out_shape=(
@@ -369,7 +413,9 @@
             jax.ShapeDtypeStruct((4, size, size), F32),
             jax.ShapeDtypeStruct((4, slots, size), F32),
         ),
-        scratch_shapes=[pltpu.VMEM((size, slots), F32)] * 6
+        out_specs=(whole,) * 5 + (pl.BlockSpec(memory_space=pl.ANY), whole),
+        scratch_shapes=[pltpu.VMEM((4, size, size), F32)]
+        + [pltpu.VMEM((size, slots), F32)] * 6
         + [pltpu.VMEM((slots, slots), F32)] * 2
         + [
             pltpu.VMEM((size, size + 3 * slots), F32),
@@ -384,9 +430,10 @@
             pltpu.SemaphoreType.DMA((6, count)),
             pltpu.SemaphoreType.DMA((2,)),
             pltpu.SemaphoreType.DMA((2,)),
+            pltpu.SemaphoreType.DMA((4, count // 2)),
         ],
         compiler_params=pltpu.CompilerParams(
-            vmem_limit_bytes=56 * 2**20, collective_id=0, has_side_effects=True
+            vmem_limit_bytes=60 * 2**20, collective_id=0, has_side_effects=True
         ),
         cost_estimate=pl.CostEstimate(
             flops=30 * size * size * size, bytes_accessed=30 * size * size, transcendentals=0
@@ -396,8 +443,8 @@
 
 
 def last_kernel(
-    flag_ref, recv_ref, ath_ref, atl_ref, q_ref, shift_ref, l_ref, w1_ref, w2_ref, c_ref, f_ref,
-    schur_ref, coup_ref, qh_ref, ql_ref, sem,
+    flag_ref, recv_ref, ath_ref, atl_ref, qin_ref, shift_ref, lin_ref, w1_ref, w2_ref, cin_ref, f_ref,
+    schur_ref, coup_ref, q_ref, l_ref, c_ref, qh_ref, ql_ref, sem, in_sem, out_sem,
 ):
     step = pl.program_id(0)
     size = shift_ref.shape[1]
@@ -405,26 +452,54 @@
     half = slots // 2
     cols = schur_ref.shape[3]
     fm2, fm1, own = [flag_ref[i] > 0 for i in range(3)]
-    out = pltpu.make_async_copy(c_ref, coup_ref.at[0], sem)
+    get_q = pltpu.make_async_copy(qin_ref, q_ref, sem.at[0])
+    get_l = pltpu.make_async_copy(lin_ref, l_ref, sem.at[1])
+    get_c = [pltpu.make_async_copy(cin_ref.at[i], c_ref.at[i], in_sem.at[i]) for i in range(4)]
+    put_c = [pltpu.make_async_copy(c_ref.at[i], coup_ref.at[0, i], out_sem.at[i]) for i in range(4)]
 
     @pl.when(step == 0)
     def _():
-        out.start()
+        get_q.start()
+        get_l.start()
+        for i in (2, 3, 0, 1):
+            get_c[i].start()
+
+    base = pl.multiple_of(step * cols, cols)
+    span = pl.ds(base, cols)
+
+    def at_of(i):
+        return ath_ref[:, i * slots : (i + 1) * slots], atl_ref[:, i * slots : (i + 1) * slots]
+
+    def q_of(i):
+        return qh_ref[:, i * slots : (i + 1) * slots], ql_ref[:, i * slots : (i + 1) * slots]
+
+    def y_of(i):
+        lanes = pl.ds(pl.multiple_of(i * size + base, cols), cols)
+        a = jnp.concatenate([recv_ref[:, 0, lanes], recv_ref[:, 1, lanes]], axis=0)
+        return split2(a - f_ref[i, :, span])
+
+    @pl.when(jnp.logical_not(own))
+    def _():
+        r_id = lax.broadcasted_iota(jnp.int32, (size, cols), 0)
+        c_id = lax.broadcasted_iota(jnp.int32, (size, cols), 1) + base
+        diag = jnp.where(r_id == c_id, shift_ref[:, span], 0.0)
+        schur_ref[0, 2] = (
+            dot3(at_of(0), y_of(0)) + dot3(at_of(1), y_of(1)) + dot3(at_of(2), y_of(2))
+        ) + diag
+
+    @pl.when(step == 0)
+    def _():
+        get_q.wait()
         for i in range(3):
             for s in range(2):
                 begin = i * slots + s * half
                 hi, lo = split2(q_ref[:, s, i * size : (i + 1) * size].T)
                 qh_ref[:, begin : begin + half] = hi
                 ql_ref[:, begin : begin + half] = lo
-
-    base = pl.multiple_of(step * cols, cols)
-    span = pl.ds(base, cols)
-
-    def at_of(i):
-        return ath_ref[:, i * slots : (i + 1) * slots], atl_ref[:, i * slots : (i + 1) * slots]
-
-    def q_of(i):
-        return qh_ref[:, i * slots : (i + 1) * slots], ql_ref[:, i * slots : (i + 1) * slots]
+        get_l.wait()
+        for i in (2, 3, 0, 1):
+            get_c[i].wait()
+            put_c[i].start()
 
     @pl.when(own)
     def _():
@@ -437,25 +512,13 @@
 
     @pl.when(jnp.logical_not(own))
     def _():
-        y = []
-        for i in range(3):
-            lanes = pl.ds(pl.multiple_of(i * size + base, cols), cols)
-            a = jnp.concatenate([recv_ref[:, 0, lanes], recv_ref[:, 1, lanes]], axis=0)
-            y.append(split2(a - f_ref[i, :, span]))
-        r_id = lax.broadcasted_iota(jnp.int32, (size, cols), 0)
-        c_id = lax.broadcasted_iota(jnp.int32, (size, cols), 1) + base
-        diag = jnp.where(r_id == c_id, shift_ref[:, span], 0.0)
-        schur_ref[0, 2] = (
-            dot3(at_of(0), y[0]) + dot3(at_of(1), y[1]) + dot3(at_of(2), y[2])
-        ) + diag
-
         @pl.when(fm1)
         def _():
             schur_ref[0, 1] = c_ref[2, :, span]
 
         @pl.when(jnp.logical_not(fm1))
         def _():
-            schur_ref[0, 1] = dot3(q_of(0), y[1]) + dot3(q_of(1), y[2])
+            schur_ref[0, 1] = dot3(q_of(0), y_of(1)) + dot3(q_of(1), y_of(2))
 
             @pl.when(fm2)
             def _():
@@ -467,7 +530,7 @@
 
         @pl.when(jnp.logical_not(fm2))
         def _():
-            schur_ref[0, 0] = dot3(q_of(2), y[2])
+            schur_ref[0, 0] = dot3(q_of(2), y_of(2))
 
             @pl.when(fm1)
             def _():
@@ -475,7 +538,8 @@
 
     @pl.when(step == pl.num_programs(0) - 1)
     def _():
-        out.wait()
+        for i in range(4):
+            put_c[i].wait()
 
 
 def last(flags, recv, q, shift, l, w1, w2, ath, atl, c, f):
@@ -483,24 +547,30 @@
     slots = w1.shape[1]
     cols = 256
     whole = pl.BlockSpec(memory_space=pltpu.VMEM)
+    far = pl.BlockSpec(memory_space=pl.ANY)
     return pl.pallas_call(
         last_kernel,
         grid=(size // cols,),
-        in_specs=[pl.BlockSpec(memory_space=pltpu.SMEM)] + [whole] * 10,
-        out_specs=(
-            pl.BlockSpec((1, 3, size, cols), lambda n: (0, 0, 0, n)),
-            pl.BlockSpec(memory_space=pl.ANY),
-        ),
+        in_specs=[
+            pl.BlockSpec(memory_space=pltpu.SMEM),
+            whole, whole, whole, far, whole, far, whole, whole, far, whole,
+        ],
+        out_specs=(pl.BlockSpec((1, 3, size, cols), lambda n: (0, 0, 0, n)), far),
         out_shape=(
             jax.ShapeDtypeStruct((1, 3, size, size), F32),
             jax.ShapeDtypeStruct((1, 4, size, size), F32),
         ),
         scratch_shapes=[
+            pltpu.VMEM(q.shape, F32),
+            pltpu.VMEM((size, size), F32),
+            pltpu.VMEM((4, size, size), F32),
             pltpu.VMEM((size, 3 * slots), BF16),
             pltpu.VMEM((size, 3 * slots), BF16),
-            pltpu.SemaphoreType.DMA,
+            pltpu.SemaphoreType.DMA((2,)),
+            pltpu.SemaphoreType.DMA((4,)),
+            pltpu.SemaphoreType.DMA((4,)),
         ],
-        compiler_params=pltpu.CompilerParams(vmem_limit_bytes=44 * 2**20),
+        compiler_params=pltpu.CompilerParams(vmem_limit_bytes=60 * 2**20),
         name="last",
     )(flags, recv, ath, atl, q, shift, l, w1, w2, c, f)
 

time: 177 us -> 171 us (0.966)
  local copies, waits for them, and re-layouts: 6.12 us -> 1.31 us
    unnamed x16 -> x4, local copies, waits for them, and re-layouts: 4.81 us -> 0.01 us
    pallas_call x1, Pallas kernels: 100 us -> 96.9 us  [chol(): pl.pallas_call(chol_kernel, out_shape=(jax.ShapeDtypeStruct((size, size),...]
where the time goes in v3:
time: 171 us
  Pallas kernels  124 us (73%)
  waiting for transfers between devices  27.7 us (16%)
  starting transfers between devices  17.1 us (10%)
    pallas_call x1, Pallas kernels, chol(): pl.pallas_call(chol_kernel, out_shape=(jax.ShapeDtypeStruct((size, size),...  96.9 us
    all_to_all x2, waiting for transfers between devices, exchange(): lax.all_to_all(payload, AXES, split_axis=0, concat_axis=0, tiled=True)  27.7 us
    pallas_call x1, Pallas kernels, last(): pl.pallas_call(last_kernel, grid=(size // cols,), in_specs=[pl.BlockSpec(...  18 us
    all_to_all x2, starting transfers between devices, exchange(): lax.all_to_all(payload, AXES, split_axis=0, concat_axis=0, tiled=True)  17.1 us
    pallas_call x2, Pallas kernels, bucket(): pl.pallas_call(kernel, out_shape=jax.ShapeDtypeStruct((n, 2, wide), F32),...  8.71 us
  transfers between devices with their start and end apart: 2, of which 1 were waited for; matrix products, arithmetic and copies ran while one was open for 1% of the time, Pallas kernels for 59%

profile of v3, /device:TPU:0, one launch (start us, length us, event | category | flops | bytes accessed | tf_op | source)
XLA Modules:
  0.0 171.2 jit_solution(4216544369965521031)
XLA Ops:
  0.6 4.0 %first.1 = f32[128,2,2304]{2,1,0:T(2,128)} custom-call(f32[3,128,768]{2,1,0:T(8,128)} %bitcast.6, s32[1,128]{1,0:T(1,128)} %bitcast.8), custom_call_target="tpu_custom_call" | custom-call | flops 377487360 | bytes 3538944 | tf_op jit(solution)/shard_map/first/pallas_call | solution.py:99
  4.7 11.2 %all-to-all-start = ((f32[128,2,2304]{2,1,0:T(2,128)}), f32[128,2,2304]{2,1,0:T(2,128)S(1)}, u32[]{:S(2)}, u32[]{:S(2)}) async-start(f32[128,2,2304]{2,1,0:T(2,128)} %first.1), calls=%async_computation | async-start | bytes 4718592 | tf_op jit(solution)/shard_map/all_to_all | solution.py:579
  15.8 4.7 %second.1 = f32[128,2,2304]{2,1,0:T(2,128)} custom-call(f32[3,128,768]{2,1,0:T(8,128)} %bitcast.7, s32[1,128]{1,0:T(1,128)} %bitcast.9, s32[1,128]{1,0:T(1,128)} %bitcast.5), custom_call_target="tpu_custom_call" | custom-call | flops 377487360 | bytes 3538944 | tf_op jit(solution)/shard_map/second/pallas_call | solution.py:99
  20.5 0.0 copy-start
  20.5 27.7 %all-to-all-done.recv_ref = f32[128,2,2304]{2,1,0:T(2,128)S(1)} async-done(((f32[128,2,2304]{2,1,0:T(2,128)}), f32[128,2,2304]{2,1,0:T(2,128)S(1)}, u32[]{:S(2)}, u32[]{:S(2)}) %all-to-all-start) | async-done | bytes 2359328 | tf_op jit(solution)/shard_map/all_to_all | solution.py:579
  48.3 0.0 copy-start.1
  48.3 5.9 %all-to-all-start.1 = ((f32[128,2,2304]{2,1,0:T(2,128)}), f32[128,2,2304]{2,1,0:T(2,128)}, u32[]{:S(2)}, u32[]{:S(2)}) async-start(f32[128,2,2304]{2,1,0:T(2,128)} %second.1), calls=%async_computation.1 | async-start | bytes 4718592 | tf_op jit(solution)/shard_map/all_to_all | solution.py:579
  54.2 0.0 copy-done.1
  54.2 0.0 copy-done
  54.3 0.6 gather_fusion
  54.9 0.6 fusion.3
  55.5 0.7 broadcast_in_dim.4.flag_ref
  56.1 96.9 %chol.1 = (f32[768,768]{1,0:T(8,128)}, f32[768,256]{1,0:T(8,128)}, f32[768,256]{1,0:T(8,128)}, bf16[768,768]{1,0:T(8,128)(2,1)}, bf16[768,768]{1,0:T(8,128)(2,1)...) custom-call(f32[128,2,2304]{2,1,0:T(2,128)} %copy-done.1, f32[1,768]{1,0:T(1,128)} %shift_ref.3, ...), custom_call_target="tpu_custom_call" | custom-call | flops 13589544960 | bytes 17694720 | tf_op jit(solution)/shard_map/chol/pallas_call | solution.py:409
  153.0 0.0 all-to-all-done.1.qin_ref
  153.0 18.0 %last.1 = (f32[1,3,768,768]{3,2,1,0:T(8,128)}, f32[1,4,768,768]{3,2,1,0:T(8,128)}) custom-call(s32[8]{0:T(128)} %get-tuple-element.17.flag_ref, f32[128,2,2304]{2,1,0:T(2,128)} %copy-done.1, bf16[768,768]{1,0:T(8,128)(2,1)} %get-tuple-element.9.ath_ref, bf16[768,768]{1,0:T(8,128)(2,1)} %get-tuple-element.10.atl_ref, f32[128,2,2304]{2,1,0:T(2,128)} %all-to-all-done.1.qin_ref, ...), custom_call_target="tpu_custom_call" | custom-call | tf_op jit(solution)/shard_map/last/pallas_call | solution.py:551
  (2 shorter events, 0.0 us)
Async XLA Ops:
  4.7 43.6 %all-to-all-start = ((f32[128,2,2304]{2,1,0:T(2,128)}), f32[128,2,2304]{2,1,0:T(2,128)S(1)}, u32[]{:S(2)}, u32[]{:S(2)}) async-start(f32[128,2,2304]{2,1,0:T(2,128)} %first.1), calls=%async_computation | async-start | bytes 4718592 | tf_op jit(solution)/shard_map/all_to_all | solution.py:579
  20.5 33.7 %copy-start = (s32[128]{0:T(128)S(1)}, s32[128]{0:T(128)}, u32[]{:S(2)}) copy-start(s32[128]{0:T(128)} %param.7) | copy-start | bytes 1540
  48.3 6.0 %copy-start.1 = (f32[128,2,2304]{2,1,0:T(2,128)}, f32[128,2,2304]{2,1,0:T(2,128)S(1)}, u32[]{:S(2)}) copy-start(f32[128,2,2304]{2,1,0:T(2,128)S(1)} %all-to-all-done.recv_ref) | copy-start | bytes 7077892
  48.3 104.8 %all-to-all-start.1 = ((f32[128,2,2304]{2,1,0:T(2,128)}), f32[128,2,2304]{2,1,0:T(2,128)}, u32[]{:S(2)}, u32[]{:S(2)}) async-start(f32[128,2,2304]{2,1,0:T(2,128)} %second.1), calls=%async_computation.1 | async-start | bytes 4718592 | tf_op jit(solution)/shard_map/all_to_all | solution.py:579

commit v4 on v3

--- a/solution.py
+++ b/solution.py
@@ -69,7 +69,7 @@
             out_ref[:, slot, i * width : (i + 1) * width] = pick(as_mask(hit[i]), pieces[i])
 
 
-def second_kernel(strips_ref, row_ref, flag_ref, out_ref):
+def second_kernel(strips_ref, row_ref, flag_ref, out_ref, near_ref, nearf_ref):
     width = strips_ref.shape[2]
     n = row_ref.shape[1]
     pieces = pieces_of(strips_ref)
@@ -81,6 +81,14 @@
         chosen = c_id == ((r_id + (n - step)) & (n - 1))
         return jnp.sum(jnp.where(chosen, flags, 0), axis=1, keepdims=True) > 0
 
+    own = lax.axis_index("gx") * lax.axis_size("gy") + lax.axis_index("gy")
+    t_id = lax.broadcasted_iota(jnp.int32, (8, n), 0)
+    l_id = lax.broadcasted_iota(jnp.int32, (8, n), 1)
+    chosen = l_id == ((t_id + own + (n - 2)) & (n - 1))
+    near = jnp.sum(jnp.where(chosen, flags, 0), axis=1, keepdims=True)
+    near = jnp.broadcast_to(near, (8, n))
+    near_ref[...] = near
+    nearf_ref[...] = near.astype(F32)
     one_before = flag_before(1)
     two_before = flag_before(2)
     for slot in range(2):
@@ -94,15 +102,14 @@
         ) + pick(as_mask(hit[3] & two_before), pieces[2])
 
 
-def bucket(kernel, name, *args):
+def bucket(kernel, extra, *args):
     n, wide = args[0].shape[1], 3 * args[0].shape[2]
     return pl.pallas_call(
         kernel,
-        out_shape=jax.ShapeDtypeStruct((n, 2, wide), F32),
+        out_shape=(jax.ShapeDtypeStruct((n, 2, wide), F32),) + extra,
         cost_estimate=pl.CostEstimate(
             flops=10 * n * n * wide, bytes_accessed=12 * n * wide, transcendentals=0
         ),
-        name=name,
     )(*args)
 
 
@@ -161,11 +168,11 @@
 
 def chol_kernel(
     recv_ref, shift_ref, flag_ref,
-    l_ref, w1_ref, w2_ref, ath_ref, atl_ref, cout_ref, f_ref,
-    c_ref,
+    lout_ref, w1out_ref, w2out_ref, athout_ref, atlout_ref, cout_ref, f_ref,
+    l_ref, w1_ref, w2_ref, ath_ref, atl_ref, c_ref,
     m1w0_ref, m1w1_ref, m2w0_ref, p1w1_ref, p1w2_ref, p2w2_ref, gx_ref, gy_ref,
     m_ref, x_ref, w0_ref, ah_ref, al_ref, outx_ref, outy_ref, gram_ref,
-    send_sem, recv_sem, small_send, small_recv, c_sem,
+    send_sem, recv_sem, small_send, small_recv, c_sem, o_sem,
 ):
     size = shift_ref.shape[1]
     slots = w0_ref.shape[1]
@@ -215,6 +222,16 @@
             device_id=up_id,
             device_id_type=MESH,
         )
+
+    early = [
+        pltpu.make_async_copy(source, target, o_sem.at[i])
+        for i, (source, target) in enumerate(
+            (
+                (ath_ref, athout_ref), (atl_ref, atlout_ref),
+                (l_ref, lout_ref), (w1_ref, w1out_ref), (w2_ref, w2out_ref),
+            )
+        )
+    ]
 
     def relay(k):
         copy(0, k).wait_recv()
@@ -250,6 +267,8 @@
         m_ref[0 : blk + 256, blk : blk + 256] = total + jnp.where(
             r_id == c_id, shift_ref[:, blk : blk + 256], 0.0
         )
+    for i in range(2):
+        early[i].start()
     pl.semaphore_wait(barrier, 2)
 
     w_refs = (w0_ref, w1_ref, w2_ref)
@@ -357,6 +376,8 @@
         return carry
 
     lax.fori_loop(0, count // 2, near, 0)
+    for i in range(2, 5):
+        early[i].start()
     outy_ref[...] = gram_ref[1] * flag[2] + gram_ref[2] * (1.0 - flag[2])
 
     def far(k, carry):
@@ -389,6 +410,8 @@
     for which in range(4):
         for k in range(count // 2):
             out_copy(which, k).wait()
+    for i in range(5):
+        early[i].wait()
 
     def drain(k, carry):
         for which in range(6):
@@ -403,7 +426,6 @@
     slots = 2 * recv.shape[0]
     w = jax.ShapeDtypeStruct((size, slots), F32)
     low = jax.ShapeDtypeStruct((size, 3 * slots), BF16)
-    square = jax.ShapeDtypeStruct((slots, slots), F32)
     count = size // 128
     whole = pl.BlockSpec(memory_space=pltpu.VMEM)
     return pl.pallas_call(
@@ -413,8 +435,15 @@
             jax.ShapeDtypeStruct((4, size, size), F32),
             jax.ShapeDtypeStruct((4, slots, size), F32),
         ),
-        out_specs=(whole,) * 5 + (pl.BlockSpec(memory_space=pl.ANY), whole),
-        scratch_shapes=[pltpu.VMEM((4, size, size), F32)]
+        out_specs=(pl.BlockSpec(memory_space=pl.ANY),) * 6 + (whole,),
+        scratch_shapes=[
+            pltpu.VMEM((size, size), F32),
+            pltpu.VMEM((size, slots), F32),
+            pltpu.VMEM((size, slots), F32),
+            pltpu.VMEM((size, 3 * slots), BF16),
+            pltpu.VMEM((size, 3 * slots), BF16),
+            pltpu.VMEM((4, size, size), F32),
+        ]
         + [pltpu.VMEM((size, slots), F32)] * 6
         + [pltpu.VMEM((slots, slots), F32)] * 2
         + [
@@ -431,6 +460,7 @@
             pltpu.SemaphoreType.DMA((2,)),
             pltpu.SemaphoreType.DMA((2,)),
             pltpu.SemaphoreType.DMA((4, count // 2)),
+            pltpu.SemaphoreType.DMA((5,)),
         ],
         compiler_params=pltpu.CompilerParams(
             vmem_limit_bytes=60 * 2**20, collective_id=0, has_side_effects=True
@@ -443,24 +473,33 @@
 
 
 def last_kernel(
-    flag_ref, recv_ref, ath_ref, atl_ref, qin_ref, shift_ref, lin_ref, w1_ref, w2_ref, cin_ref, f_ref,
-    schur_ref, coup_ref, q_ref, l_ref, c_ref, qh_ref, ql_ref, sem, in_sem, out_sem,
+    flag_ref, recv_ref, ath_ref, atl_ref, qin_ref, shift_ref, lin_ref, w1in_ref, w2in_ref, cin_ref, f_ref,
+    schur_ref, coup_ref, q_ref, l_ref, w1_ref, w2_ref, c_ref, qh_ref, ql_ref, sem, in_sem, out_sem,
 ):
     step = pl.program_id(0)
     size = shift_ref.shape[1]
     slots = w1_ref.shape[1]
     half = slots // 2
     cols = schur_ref.shape[3]
-    fm2, fm1, own = [flag_ref[i] > 0 for i in range(3)]
+    fm2, fm1, own = [flag_ref[i, 0] > 0 for i in range(3)]
     get_q = pltpu.make_async_copy(qin_ref, q_ref, sem.at[0])
-    get_l = pltpu.make_async_copy(lin_ref, l_ref, sem.at[1])
+    get_own = [
+        pltpu.make_async_copy(lin_ref, l_ref, sem.at[1]),
+        pltpu.make_async_copy(w1in_ref, w1_ref, sem.at[2]),
+        pltpu.make_async_copy(w2in_ref, w2_ref, sem.at[3]),
+    ]
     get_c = [pltpu.make_async_copy(cin_ref.at[i], c_ref.at[i], in_sem.at[i]) for i in range(4)]
     put_c = [pltpu.make_async_copy(c_ref.at[i], coup_ref.at[0, i], out_sem.at[i]) for i in range(4)]
 
     @pl.when(step == 0)
     def _():
         get_q.start()
-        get_l.start()
+
+        @pl.when(own)
+        def _():
+            for one in get_own:
+                one.start()
+
         for i in (2, 3, 0, 1):
             get_c[i].start()
 
@@ -496,7 +535,12 @@
                 hi, lo = split2(q_ref[:, s, i * size : (i + 1) * size].T)
                 qh_ref[:, begin : begin + half] = hi
                 ql_ref[:, begin : begin + half] = lo
-        get_l.wait()
+
+        @pl.when(own)
+        def _():
+            for one in get_own:
+                one.wait()
+
         for i in (2, 3, 0, 1):
             get_c[i].wait()
             put_c[i].start()
@@ -553,7 +597,7 @@
         grid=(size // cols,),
         in_specs=[
             pl.BlockSpec(memory_space=pltpu.SMEM),
-            whole, whole, whole, far, whole, far, whole, whole, far, whole,
+            whole, whole, whole, far, whole, far, far, far, far, whole,
         ],
         out_specs=(pl.BlockSpec((1, 3, size, cols), lambda n: (0, 0, 0, n)), far),
         out_shape=(
@@ -563,10 +607,12 @@
         scratch_shapes=[
             pltpu.VMEM(q.shape, F32),
             pltpu.VMEM((size, size), F32),
+            pltpu.VMEM((size, slots), F32),
+            pltpu.VMEM((size, slots), F32),
             pltpu.VMEM((4, size, size), F32),
             pltpu.VMEM((size, 3 * slots), BF16),
             pltpu.VMEM((size, 3 * slots), BF16),
-            pltpu.SemaphoreType.DMA((2,)),
+            pltpu.SemaphoreType.DMA((4,)),
             pltpu.SemaphoreType.DMA((4,)),
             pltpu.SemaphoreType.DMA((4,)),
         ],
@@ -580,17 +626,15 @@
 
 
 def local(strips, index, shift, flags):
-    count = lax.axis_size(AXES)
-    own = lax.axis_index(AXES)
     strips = jnp.transpose(strips, (1, 0, 2))
     index = index.reshape(1, -1)
-    first = bucket(first_kernel, "first", strips, index)
+    (first,) = bucket(first_kernel, (), strips, index)
+    table = (8, flags.shape[0])
+    extra = (jax.ShapeDtypeStruct(table, jnp.int32), jax.ShapeDtypeStruct(table, F32))
+    second, near, wide = bucket(second_kernel, extra, strips, index, flags.reshape(1, -1))
     recv = exchange(first)
-    second = bucket(second_kernel, "second", strips, index, flags.reshape(1, -1))
-    near = jnp.take(flags, (own + jnp.arange(-2, 6)) % count)
-    wide = jnp.broadcast_to(near.astype(F32)[:, None], (8, 128))
+    q = exchange(second)
     parts = chol(recv, shift, wide)
-    q = exchange(second)
     return last(near, recv, q, shift, *parts)
 
 

time: 171 us -> 172 us (level)
  transfers between devices with their start and end apart: 2 -> 2, of which waited for: 1 -> 1; matrix products, arithmetic and copies ran while one was open for 1% -> 0% of each run, Pallas kernels for 59% -> 59%
where the time goes in v4:
time: 172 us; the launch traced here: 171 us
  Pallas kernels  124 us (72%)
  waiting for transfers between devices  27.7 us (16%)
  starting transfers between devices  17.1 us (10%)
    pallas_call x1, Pallas kernels, chol(): pl.pallas_call(chol_kernel, out_shape=(jax.ShapeDtypeStruct((size, size),...  96.8 us
    all_to_all x2, waiting for transfers between devices, exchange(): lax.all_to_all(payload, AXES, split_axis=0, concat_axis=0, tiled=True)  27.7 us
    pallas_call x1, Pallas kernels, last(): pl.pallas_call(last_kernel, grid=(size // cols,), in_specs=[pl.BlockSpec(...  18.8 us
    all_to_all x2, starting transfers between devices, exchange(): lax.all_to_all(payload, AXES, split_axis=0, concat_axis=0, tiled=True)  17.1 us
    pallas_call x2, Pallas kernels, bucket(): pl.pallas_call(kernel, out_shape=(jax.ShapeDtypeStruct((n, 2, wide), F32)...  8.72 us
  transfers between devices with their start and end apart: 2, of which 1 were waited for; matrix products, arithmetic and copies ran while one was open for 0% of the time, Pallas kernels for 59%

profile of v4, /device:TPU:0, one launch (start us, length us, event | category | flops | bytes accessed | tf_op | source)
XLA Modules:
  0.0 171.4 jit_solution(5129502205278943756)
XLA Ops:
  0.6 4.0 %shard_map.60 = f32[128,2,2304]{2,1,0:T(2,128)} custom-call(f32[3,128,768]{2,1,0:T(8,128)} %bitcast.3, s32[1,128]{1,0:T(1,128)} %bitcast.5), custom_call_target="tpu_custom_call" | custom-call | flops 377487360 | bytes 3538944 | tf_op jit(solution)/shard_map/pallas_call | solution.py:107
  4.7 11.2 %all-to-all-start = ((f32[128,2,2304]{2,1,0:T(2,128)}), f32[128,2,2304]{2,1,0:T(2,128)S(1)}, u32[]{:S(2)}, u32[]{:S(2)}) async-start(f32[128,2,2304]{2,1,0:T(2,128)} %shard_map.60), calls=%async_computation | async-start | bytes 4718592 | tf_op jit(solution)/shard_map/all_to_all | solution.py:625
  15.8 4.7 %shard_map.59 = (f32[128,2,2304]{2,1,0:T(2,128)}, s32[8,128]{1,0:T(8,128)}, f32[8,128]{1,0:T(8,128)}) custom-call(f32[3,128,768]{2,1,0:T(8,128)} %bitcast.4, s32[1,128]{1,0:T(1,128)} %bitcast.6, s32[1,128]{1,0:T(1,128)} %bitcast.7), custom_call_target="tpu_custom_call" | custom-call | flops 377487360 | bytes 3538944 | tf_op jit(solution)/shard_map/pallas_call | solution.py:107
  20.5 27.7 %all-to-all-done.recv_ref = f32[128,2,2304]{2,1,0:T(2,128)S(1)} async-done(((f32[128,2,2304]{2,1,0:T(2,128)}), f32[128,2,2304]{2,1,0:T(2,128)S(1)}, u32[]{:S(2)}, u32[]{:S(2)}) %all-to-all-start) | async-done | bytes 2359328 | tf_op jit(solution)/shard_map/all_to_all | solution.py:625
  48.3 0.0 copy-start
  48.3 1.4 copy-done
  49.6 5.9 %all-to-all-start.1 = ((f32[128,2,2304]{2,1,0:T(2,128)}), f32[128,2,2304]{2,1,0:T(2,128)}, u32[]{:S(2)}, u32[]{:S(2)}) async-start(f32[128,2,2304]{2,1,0:T(2,128)} %get-tuple-element.16), calls=%async_computation.1 | async-start | bytes 4718592 | tf_op jit(solution)/shard_map/all_to_all | solution.py:625
  55.5 96.8 %chol.1 = (f32[768,768]{1,0:T(8,128)}, f32[768,256]{1,0:T(8,128)}, f32[768,256]{1,0:T(8,128)}, bf16[768,768]{1,0:T(8,128)(2,1)}, bf16[768,768]{1,0:T(8,128)(2,1)...) custom-call(f32[128,2,2304]{2,1,0:T(2,128)} %copy-done, f32[1,768]{1,0:T(1,128)} %shift_ref.3, ...), custom_call_target="tpu_custom_call" | custom-call | flops 13589544960 | bytes 17694720 | tf_op jit(solution)/shard_map/chol/pallas_call | solution.py:431
  152.4 0.0 all-to-all-done.1.qin_ref
  152.4 18.8 %last.1 = (f32[1,3,768,768]{3,2,1,0:T(8,128)}, f32[1,4,768,768]{3,2,1,0:T(8,128)}) custom-call(s32[8,128]{1,0:T(8,128)} %get-tuple-element.12.flag_ref, f32[128,2,2304]{2,1,0:T(2,128)} %copy-done, bf16[768,768]{1,0:T(8,128)(2,1)} %get-tuple-element.14.ath_ref, bf16[768,768]{1,0:T(8,128)(2,1)} %get-tuple-element.15.atl_ref, ...), custom_call_target="tpu_custom_call" | custom-call | tf_op jit(solution)/shard_map/last/pallas_call | solution.py:595
Async XLA Ops:
  4.7 43.6 %all-to-all-start = ((f32[128,2,2304]{2,1,0:T(2,128)}), f32[128,2,2304]{2,1,0:T(2,128)S(1)}, u32[]{:S(2)}, u32[]{:S(2)}) async-start(f32[128,2,2304]{2,1,0:T(2,128)} %shard_map.60), calls=%async_computation | async-start | bytes 4718592 | tf_op jit(solution)/shard_map/all_to_all | solution.py:625
  48.3 1.4 copy-start
  49.6 102.8 %all-to-all-start.1 = ((f32[128,2,2304]{2,1,0:T(2,128)}), f32[128,2,2304]{2,1,0:T(2,128)}, u32[]{:S(2)}, u32[]{:S(2)}) async-start(f32[128,2,2304]{2,1,0:T(2,128)} %get-tuple-element.16), calls=%async_computation.1 | async-start | bytes 4718592 | tf_op jit(solution)/shard_map/all_to_all | solution.py:625

commit v5 on v4

--- a/solution.py
+++ b/solution.py
@@ -63,10 +63,13 @@
 def first_kernel(strips_ref, row_ref, out_ref):
     width = strips_ref.shape[2]
     pieces = pieces_of(strips_ref)
-    for slot in range(2):
-        hit = hits_of(row_ref[...], slot)
-        for i in range(3):
-            out_ref[:, slot, i * width : (i + 1) * width] = pick(as_mask(hit[i]), pieces[i])
+    n = row_ref.shape[1]
+    hits = [hits_of(row_ref[...], slot) for slot in range(2)]
+    for i in range(3):
+        both = jnp.concatenate([as_mask(hit[i]) for hit in hits], axis=0)
+        rows = pick(both, pieces[i])
+        for slot in range(2):
+            out_ref[:, slot, i * width : (i + 1) * width] = rows[slot * n : (slot + 1) * n]
 
 
 def second_kernel(strips_ref, row_ref, flag_ref, out_ref, near_ref, nearf_ref):
@@ -110,6 +113,7 @@
         cost_estimate=pl.CostEstimate(
             flops=10 * n * n * wide, bytes_accessed=12 * n * wide, transcendentals=0
         ),
+        compiler_params=pltpu.CompilerParams(vmem_limit_bytes=62 * 2**20),
     )(*args)
 
 
@@ -463,7 +467,7 @@
             pltpu.SemaphoreType.DMA((5,)),
         ],
         compiler_params=pltpu.CompilerParams(
-            vmem_limit_bytes=60 * 2**20, collective_id=0, has_side_effects=True
+            vmem_limit_bytes=62 * 2**20, collective_id=0, has_side_effects=True
         ),
         cost_estimate=pl.CostEstimate(
             flops=30 * size * size * size, bytes_accessed=30 * size * size, transcendentals=0
@@ -616,7 +620,7 @@
             pltpu.SemaphoreType.DMA((4,)),
             pltpu.SemaphoreType.DMA((4,)),
         ],
-        compiler_params=pltpu.CompilerParams(vmem_limit_bytes=60 * 2**20),
+        compiler_params=pltpu.CompilerParams(vmem_limit_bytes=62 * 2**20),
         name="last",
     )(flags, recv, ath, atl, q, shift, l, w1, w2, c, f)
 

time: 172 us -> 171 us (level)
  transfers between devices with their start and end apart: 2 -> 2, of which waited for: 1 -> 1; matrix products, arithmetic and copies ran while one was open for 0% -> 0% of each run, Pallas kernels for 59% -> 60%
where the time goes in v5:
time: 171 us; the launch traced here: 170 us
  Pallas kernels  124 us (73%)
  waiting for transfers between devices  27.4 us (16%)
  starting transfers between devices  17.5 us (10%)
    pallas_call x1, Pallas kernels, chol(): pl.pallas_call(chol_kernel, out_shape=(jax.ShapeDtypeStruct((size, size),...  96.8 us
    all_to_all x2, waiting for transfers between devices, exchange(): lax.all_to_all(payload, AXES, split_axis=0, concat_axis=0, tiled=True)  27.4 us
    pallas_call x1, Pallas kernels, last(): pl.pallas_call(last_kernel, grid=(size // cols,), in_specs=[pl.BlockSpec(...  18.8 us
    all_to_all x2, starting transfers between devices, exchange(): lax.all_to_all(payload, AXES, split_axis=0, concat_axis=0, tiled=True)  17.5 us
    pallas_call x2, Pallas kernels, bucket(): pl.pallas_call(kernel, out_shape=(jax.ShapeDtypeStruct((n, 2, wide), F32)...  8.86 us
  transfers between devices with their start and end apart: 2, of which 1 were waited for; matrix products, arithmetic and copies ran while one was open for 0% of the time, Pallas kernels for 60%

profile of v5, /device:TPU:0, one launch (start us, length us, event | category | flops | bytes accessed | tf_op | source)
XLA Modules:
  0.0 170.3 jit_solution(10351723604152823290)
XLA Ops:
  0.6 4.2 %shard_map.60 = f32[128,2,2304]{2,1,0:T(2,128)} custom-call(f32[3,128,768]{2,1,0:T(8,128)} %bitcast.3, s32[1,128]{1,0:T(1,128)} %bitcast.5), custom_call_target="tpu_custom_call" | custom-call | flops 377487360 | bytes 3538944 | tf_op jit(solution)/shard_map/pallas_call | solution.py:110
  4.8 11.6 %all-to-all-start = ((f32[128,2,2304]{2,1,0:T(2,128)}), f32[128,2,2304]{2,1,0:T(2,128)}, u32[]{:S(2)}, u32[]{:S(2)}) async-start(f32[128,2,2304]{2,1,0:T(2,128)} %shard_map.60), calls=%async_computation | async-start | bytes 4718592 | tf_op jit(solution)/shard_map/all_to_all | solution.py:629
  16.5 4.7 %shard_map.59 = (f32[128,2,2304]{2,1,0:T(2,128)}, s32[8,128]{1,0:T(8,128)}, f32[8,128]{1,0:T(8,128)}) custom-call(f32[3,128,768]{2,1,0:T(8,128)} %bitcast.4, s32[1,128]{1,0:T(1,128)} %bitcast.6, s32[1,128]{1,0:T(1,128)} %bitcast.7), custom_call_target="tpu_custom_call" | custom-call | flops 377487360 | bytes 3538944 | tf_op jit(solution)/shard_map/pallas_call | solution.py:110
  21.1 27.4 %all-to-all-done.recv_ref = f32[128,2,2304]{2,1,0:T(2,128)} async-done(((f32[128,2,2304]{2,1,0:T(2,128)}), f32[128,2,2304]{2,1,0:T(2,128)}, u32[]{:S(2)}, u32[]{:S(2)}) %all-to-all-start) | async-done | bytes 2359328 | tf_op jit(solution)/shard_map/all_to_all | solution.py:629
  48.5 5.9 %all-to-all-start.1 = ((f32[128,2,2304]{2,1,0:T(2,128)}), f32[128,2,2304]{2,1,0:T(2,128)}, u32[]{:S(2)}, u32[]{:S(2)}) async-start(f32[128,2,2304]{2,1,0:T(2,128)} %get-tuple-element.16), calls=%async_computation.1 | async-start | bytes 4718592 | tf_op jit(solution)/shard_map/all_to_all | solution.py:629
  54.4 96.8 %chol.1 = (f32[768,768]{1,0:T(8,128)}, f32[768,256]{1,0:T(8,128)}, f32[768,256]{1,0:T(8,128)}, bf16[768,768]{1,0:T(8,128)(2,1)}, bf16[768,768]{1,0:T(8,128)(2,1)...) custom-call(f32[128,2,2304]{2,1,0:T(2,128)} %all-to-all-done.recv_ref, f32[1,768]{1,0:T(1,128)} %shift_ref.3, ...), custom_call_target="tpu_custom_call" | custom-call | flops 13589544960 | bytes 17694720 | tf_op jit(solution)/shard_map/chol/pallas_call | solution.py:435
  151.2 0.0 all-to-all-done.1.qin_ref
  151.2 18.8 %last.1 = (f32[1,3,768,768]{3,2,1,0:T(8,128)}, f32[1,4,768,768]{3,2,1,0:T(8,128)}) custom-call(s32[8,128]{1,0:T(8,128)} %get-tuple-element.12.flag_ref, f32[128,2,2304]{2,1,0:T(2,128)} %all-to-all-done.recv_ref, bf16[768,768]{1,0:T(8,128)(2,1)} %get-tuple-element.14.ath_ref, bf16[768,768]{1,0:T(8,128)(2,1)} %get-tuple-element.15.atl_ref, ...), custom_call_target="tpu_custom_call" | custom-call | tf_op jit(solution)/shard_map/last/pallas_call | solution.py:599
Async XLA Ops:
  4.8 43.7 %all-to-all-start = ((f32[128,2,2304]{2,1,0:T(2,128)}), f32[128,2,2304]{2,1,0:T(2,128)}, u32[]{:S(2)}, u32[]{:S(2)}) async-start(f32[128,2,2304]{2,1,0:T(2,128)} %shard_map.60), calls=%async_computation | async-start | bytes 4718592 | tf_op jit(solution)/shard_map/all_to_all | solution.py:629
  48.5 102.7 %all-to-all-start.1 = ((f32[128,2,2304]{2,1,0:T(2,128)}), f32[128,2,2304]{2,1,0:T(2,128)}, u32[]{:S(2)}, u32[]{:S(2)}) async-start(f32[128,2,2304]{2,1,0:T(2,128)} %get-tuple-element.16), calls=%async_computation.1 | async-start | bytes 4718592 | tf_op jit(solution)/shard_map/all_to_all | solution.py:629
